TPU v7x, 32 devices: a 4x4x1 block of a 4x4x8 slice. The times are simulated.
32 devices in a mesh: batch: 1 (over z), row: 4 (over y), col: 8 (over x, core).
Axes of the slice: x: 4, y: 4, z: 1, core: 2. Of those that a mesh axis runs over, the one named last changes fastest.
The devices are a block of a 4x4x8 slice.
Arguments:
- lower_tri: bfloat16 [14336, 14336], P(('batch', 'row'), 'col')
- right_side: bfloat16 [14336, 4096], P(('batch', 'row'), 'col')
- grad_out: bfloat16 [14336, 4096], P(('batch', 'row'), 'col')
Outputs:
- output 1: bfloat16 [14336, 4096], P(('batch', 'row'), 'col')
- output 2: bfloat16 [14336, 14336], P(('batch', 'row'), 'col')
All inputs are finite; a program needn't handle non-finite values.
Results may differ from a plain program's by a relative error of at most 0.001.
Values are sent between devices in bfloat16 or wider.
A program may use at most 768 MiB of HBM per device.

v0:
```python
import jax
import jax.numpy as jnp
from jax import lax
from jax.sharding import PartitionSpec as P

BLOCK_SIZE = 256


def solution(mesh):
    mesh_rows = mesh.shape["row"]
    mesh_cols = mesh.shape["col"]
    group_size = max(mesh_rows, mesh_cols)
    row_step = group_size // mesh_rows
    col_step = group_size // mesh_cols
    block_spec = P(("batch", "row"), "col")

    def per_device(lower_tri, right_side, grad_out):
        rows_here, cols_here = lower_tri.shape
        num_cols = right_side.shape[1]
        num_steps = rows_here // (row_step * BLOCK_SIZE)
        right_pieces = []
        lower_pieces = []
        for step_idx in range(num_steps):
            first_row = step_idx * row_step * BLOCK_SIZE
            left_rows = rows_here - first_row
            grad_rows = grad_out[first_row:]
            lower_panel = lower_tri[first_row:, step_idx * col_step * BLOCK_SIZE:(step_idx + 1) * col_step * BLOCK_SIZE]
            gathered = lax.all_gather(lower_panel.reshape(left_rows, col_step, BLOCK_SIZE), "col", axis=2)
            right_part = jnp.einsum("rbqe,rf->bqef", gathered, grad_rows, preferred_element_type=jnp.float32)
            right_mine = lax.psum_scatter(right_part.reshape(row_step, mesh_rows * BLOCK_SIZE, num_cols), "row", scatter_dimension=1, tiled=True)
            right_pieces.append(right_mine.reshape(row_step * BLOCK_SIZE, num_cols).astype(jnp.bfloat16))
            side_block = right_side[first_row:first_row + row_step * BLOCK_SIZE].reshape(row_step, BLOCK_SIZE, num_cols)
            side_rows = lax.all_gather(side_block, "row", axis=1).reshape(col_step, mesh_cols, BLOCK_SIZE, num_cols)
            lower_part = jnp.einsum("rf,bqef->rbqe", grad_rows, side_rows, preferred_element_type=jnp.float32)
            lower_mine = lax.psum_scatter(lower_part.reshape(left_rows, col_step, mesh_cols * BLOCK_SIZE), "col", scatter_dimension=2, tiled=True)
            lower_piece = lower_mine.reshape(left_rows, col_step * BLOCK_SIZE).astype(jnp.bfloat16)
            lower_pieces.append(jnp.pad(lower_piece, ((first_row, 0), (0, 0))))
        grad_right = jnp.concatenate(right_pieces, axis=0)
        grad_lower = jnp.concatenate(lower_pieces, axis=1)
        row_pos = jnp.arange(rows_here)[:, None]
        col_pos = jnp.arange(cols_here)[None, :]
        row_global = (row_pos // BLOCK_SIZE * mesh_rows + lax.axis_index("row")) * BLOCK_SIZE + row_pos % BLOCK_SIZE
        col_global = (col_pos // BLOCK_SIZE * mesh_cols + lax.axis_index("col")) * BLOCK_SIZE + col_pos % BLOCK_SIZE
        grad_lower = jnp.where(row_global >= col_global, grad_lower, 0.0).astype(jnp.bfloat16)
        return grad_right, grad_lower

    return jax.shard_map(per_device, mesh=mesh, in_specs=(block_spec, block_spec, block_spec), out_specs=(block_spec, block_spec), check_vma=False)
```

profile of v0, /device:TPU:97, one launch (start us, length us, event | category | flops | bytes accessed | tf_op | source)
XLA Modules:
  0.0 1579.3 jit_solution(2365295186221135021)
XLA Ops:
  7.2 3.8 fusion.48
  11.2 1.7 slice.71
  13.0 1.9 slice.69
  15.0 2.1 slice.67
  17.9 2.3 slice.65
  20.3 2.5 slice.63
  23.8 2.7 slice.61
  26.6 2.8 slice.60
  32.4 10.6 all-gather.34.cloned.1.call-done
  43.0 5.0 convolution_bitcast_fusion.6
  48.2 20.9 %all-gather.48.cloned.1.call-done = bf16[512,2048]{1,0:T(8,128)(2,1)} async-done(((bf16[512,256]{1,0:T(8,128)(2,1)}), bf16[512,2048]{1,0:T(8,128)(2,1)}) %all-gather.48.cloned.1.call-update) | async-done | bytes 2097168 | tf_op jit(solution)/shard_map/all_gather | solution.py:28
  69.1 2.9 copy.25
  71.9 4.3 fusion.22
  76.3 28.2 %all-gather.46.cloned.1.call-done = bf16[1024,2048]{1,0:T(8,128)(2,1)} async-done(((bf16[1024,256]{1,0:T(8,128)(2,1)}), bf16[1024,2048]{1,0:T(8,128)(2,1)}) %all-gather.46.cloned.1.call-update) | async-done | bytes 4194320 | tf_op jit(solution)/shard_map/all_gather | solution.py:28
  104.5 6.4 copy.24
  110.9 6.9 fusion.18
  117.9 30.2 %all-gather.44.cloned.1.call-done = bf16[1536,2048]{1,0:T(8,128)(2,1)} async-done(((bf16[1536,256]{1,0:T(8,128)(2,1)}), bf16[1536,2048]{1,0:T(8,128)(2,1)}) %all-gather.44.cloned.1.call-update) | async-done | bytes 6291472 | tf_op jit(solution)/shard_map/all_gather | solution.py:28
  148.1 8.6 copy.23
  156.7 8.6 fusion.14
  165.5 12.4 all-gather.32.cloned.1.call-done
  177.9 7.5 convolution_bitcast_fusion.5
  185.7 44.5 %all-gather.42.cloned.1.call-done = bf16[2048,2048]{1,0:T(8,128)(2,1)} async-done(((bf16[2048,256]{1,0:T(8,128)(2,1)}), bf16[2048,2048]{1,0:T(8,128)(2,1)}) %all-gather.42.cloned.1.call-update) | async-done | bytes 8388624 | tf_op jit(solution)/shard_map/all_gather | solution.py:28
  230.3 12.2 copy.22
  242.5 10.5 fusion.10
  253.1 39.2 %all-gather.40.cloned.1.call-done = bf16[2560,2048]{1,0:T(8,128)(2,1)} async-done(((bf16[2560,256]{1,0:T(8,128)(2,1)}), bf16[2560,2048]{1,0:T(8,128)(2,1)}) %all-gather.40.cloned.1.call-update) | async-done | bytes 10485776 | tf_op jit(solution)/shard_map/all_gather | solution.py:28
  292.3 13.7 copy.21
  306.0 11.6 fusion.6
  317.7 4.5 all-gather.30.cloned.1.call-done
  322.2 10.0 convolution_bitcast_fusion.3
  332.6 60.6 %all-gather.38.cloned.1.call-done = bf16[3072,2048]{1,0:T(8,128)(2,1)} async-done(((bf16[3072,256]{1,0:T(8,128)(2,1)}), bf16[3072,2048]{1,0:T(8,128)(2,1)}) %all-gather.38.cloned.1.call-update) | async-done | bytes 12582928 | tf_op jit(solution)/shard_map/all_gather | solution.py:28
  393.2 16.6 %copy.20 = bf16[3072,2048]{0,1:T(8,128)(2,1)} copy(bf16[3072,2048]{1,0:T(8,128)(2,1)} %all-gather.38.cloned.1.call-done) | data formatting | bytes 25165824 | tf_op jit(solution)/shard_map/reshape.3
  409.8 11.9 fusion.2
  421.8 52.2 %all-gather.36.cloned.1.call-done = bf16[3584,2048]{1,0:T(8,128)(2,1)} async-done(((bf16[3584,256]{1,0:T(8,128)(2,1)}), bf16[3584,2048]{1,0:T(8,128)(2,1)}) %all-gather.36.cloned.1.call-update) | async-done | bytes 14680080 | tf_op jit(solution)/shard_map/all_gather | solution.py:28
  474.0 18.7 %copy.19 = bf16[3584,2048]{0,1:T(8,128)(2,1)} copy(bf16[3584,2048]{1,0:T(8,128)(2,1)} %all-gather.36.cloned.1.call-done) | data formatting | bytes 29360128 | tf_op jit(solution)/shard_map/reshape
  492.8 13.3 fusion
  506.3 12.6 convolution_bitcast_fusion.4
  519.2 14.2 all-gather.26.cloned.1.call-done
  533.4 12.2 convolution_bitcast_fusion.1
  545.8 17.2 %all-gather.24.cloned.1.call-done = bf16[2,4,256,512]{3,2,1,0:T(8,128)(2,1)} async-done(((bf16[2,1,256,512]{3,2,1,0:T(8,128)(2,1)}), bf16[2,4,256,512]{3,2,1,0:T(8,128)(2,1)}) %all-gather.24.cloned.1.call-update) | async-done | bytes 2097168 | tf_op jit(solution)/shard_map/all_gather | solution.py:33
  563.0 14.1 convolution_bitcast_fusion.2
  577.6 14.9 all-gather.22.cloned.1.call-done
  592.5 15.9 %convolution_bitcast_fusion = f32[3584,1,2048]{2,0,1:T(8,128)} fusion(bf16[3584,512]{1,0:T(8,128)(2,1)} %param.5, bf16[2048,512]{1,0:T(8,128)(2,1)} %bitcast.141), kind=kOutput, calls=%fused_computation.1 | convolution fusion | flops 7516192768 | bytes 35127296 | tf_op jit(solution)/shard_map/rf,bqef->rbqe/dot_general | solution.py:34
  608.5 18.8 %reduce-scatter.41.cloned.1.call-done = f32[512,1,256]{2,0,1:T(8,128)} async-done(((f32[512,1,2048]{2,0,1:T(8,128)}), f32[512,1,256]{2,0,1:T(8,128)}) %reduce-scatter.41.cloned.1.call-update) | async-done | bytes 524304 | tf_op jit(solution)/shard_map/reduce_scatter | solution.py:35
  628.4 47.0 %reduce-scatter.27.cloned.1.call-done = f32[2,256,512]{2,1,0:T(8,128)} async-done(((f32[2,1024,512]{2,1,0:T(8,128)}), f32[2,256,512]{2,1,0:T(8,128)}) %reduce-scatter.27.cloned.1.call-update) | async-done | bytes 1048592 | tf_op jit(solution)/shard_map/reduce_scatter | solution.py:30
  675.4 1.3 convert_element_type.110
  676.7 44.9 %reduce-scatter.25.cloned.1.call-done = f32[2,256,512]{2,1,0:T(8,128)} async-done(((f32[2,1024,512]{2,1,0:T(8,128)}), f32[2,256,512]{2,1,0:T(8,128)}) %reduce-scatter.25.cloned.1.call-update) | async-done | bytes 1048592 | tf_op jit(solution)/shard_map/reduce_scatter | solution.py:30
  722.9 44.9 %reduce-scatter.23.cloned.1.call-done = f32[2,256,512]{2,1,0:T(8,128)} async-done(((f32[2,1024,512]{2,1,0:T(8,128)}), f32[2,256,512]{2,1,0:T(8,128)}) %reduce-scatter.23.cloned.1.call-update) | async-done | bytes 1048592 | tf_op jit(solution)/shard_map/reduce_scatter | solution.py:30
  769.2 50.4 %reduce-scatter.39.cloned.1.call-done = f32[1024,1,256]{2,0,1:T(8,128)} async-done(((f32[1024,1,2048]{2,0,1:T(8,128)}), f32[1024,1,256]{2,0,1:T(8,128)}) %reduce-scatter.39.cloned.1.call-update) | async-done | bytes 1048592 | tf_op jit(solution)/shard_map/reduce_scatter | solution.py:35
  819.6 2.1 convert_bitcast_fusion.4
  821.7 44.4 %reduce-scatter.21.cloned.1.call-done = f32[2,256,512]{2,1,0:T(8,128)} async-done(((f32[2,1024,512]{2,1,0:T(8,128)}), f32[2,256,512]{2,1,0:T(8,128)}) %reduce-scatter.21.cloned.1.call-update) | async-done | bytes 1048592 | tf_op jit(solution)/shard_map/reduce_scatter | solution.py:30
  867.3 45.1 %reduce-scatter.19.cloned.1.call-done = f32[2,256,512]{2,1,0:T(8,128)} async-done(((f32[2,1024,512]{2,1,0:T(8,128)}), f32[2,256,512]{2,1,0:T(8,128)}) %reduce-scatter.19.cloned.1.call-update) | async-done | bytes 1048592 | tf_op jit(solution)/shard_map/reduce_scatter | solution.py:30
  913.7 70.4 %reduce-scatter.37.cloned.1.call-done = f32[1536,1,256]{2,0,1:T(8,128)} async-done(((f32[1536,1,2048]{2,0,1:T(8,128)}), f32[1536,1,256]{2,0,1:T(8,128)}) %reduce-scatter.37.cloned.1.call-update) | async-done | bytes 1572880 | tf_op jit(solution)/shard_map/reduce_scatter | solution.py:35
  984.1 2.4 convert_bitcast_fusion.3
  986.5 44.2 %reduce-scatter.17.cloned.1.call-done = f32[2,256,512]{2,1,0:T(8,128)} async-done(((f32[2,1024,512]{2,1,0:T(8,128)}), f32[2,256,512]{2,1,0:T(8,128)}) %reduce-scatter.17.cloned.1.call-update) | async-done | bytes 1048592 | tf_op jit(solution)/shard_map/reduce_scatter | solution.py:30
  1031.9 45.5 %reduce-scatter.15.cloned.1.call-done = f32[2,256,512]{2,1,0:T(8,128)} async-done(((f32[2,1024,512]{2,1,0:T(8,128)}), f32[2,256,512]{2,1,0:T(8,128)}) %reduce-scatter.15.cloned.1.call-update) | async-done | bytes 1048592 | tf_op jit(solution)/shard_map/reduce_scatter | solution.py:30
  1084.5 84.1 %reduce-scatter.35.cloned.1.call-done = f32[2048,1,256]{2,0,1:T(8,128)} async-done(((f32[2048,1,2048]{2,0,1:T(8,128)}), f32[2048,1,256]{2,0,1:T(8,128)}) %reduce-scatter.35.cloned.1.call-update) | async-done | bytes 2097168 | tf_op jit(solution)/shard_map/reduce_scatter | solution.py:35
  1168.6 2.7 convert_bitcast_fusion.2
  1171.3 108.3 %reduce-scatter.33.cloned.1.call-done = f32[2560,1,256]{2,0,1:T(8,128)} async-done(((f32[2560,1,2048]{2,0,1:T(8,128)}), f32[2560,1,256]{2,0,1:T(8,128)}) %reduce-scatter.33.cloned.1.call-update) | async-done | bytes 2621456 | tf_op jit(solution)/shard_map/reduce_scatter | solution.py:35
  1279.6 1.9 convert_bitcast_fusion.1
  1281.5 128.9 %reduce-scatter.31.cloned.1.call-done = f32[3072,1,256]{2,0,1:T(8,128)} async-done(((f32[3072,1,2048]{2,0,1:T(8,128)}), f32[3072,1,256]{2,0,1:T(8,128)}) %reduce-scatter.31.cloned.1.call-update) | async-done | bytes 3145744 | tf_op jit(solution)/shard_map/reduce_scatter | solution.py:35
  1410.4 2.0 convert_bitcast_fusion
  1412.4 148.7 %reduce-scatter.29.cloned.1.call-done = f32[3584,1,256]{2,0,1:T(8,128)} async-done(((f32[3584,1,2048]{2,0,1:T(8,128)}), f32[3584,1,256]{2,0,1:T(8,128)}) %reduce-scatter.29.cloned.1.call-update) | async-done | bytes 3670032 | tf_op jit(solution)/shard_map/reduce_scatter | solution.py:35
  1561.1 2.2 bitcast_dynamic-update-slice_fusion
  1565.2 6.7 compare_select_fusion
  (85 shorter events, 24.2 us)
Async XLA Ops:
  7.2 35.8 %all-gather.34.cloned.1.call-start = ((), (), s32[]{:S(2)}) async-start(), calls=%async_computation.33 | async-start | bytes 2621440 | tf_op jit(solution)/shard_map/all_gather | solution.py:33
  11.1 57.9 %all-gather.48.cloned.1.call-start = ((), (), s32[]{:S(2)}) async-start(), calls=%async_computation.41 | async-start | bytes 2359296 | tf_op jit(solution)/shard_map/all_gather | solution.py:28
  13.0 91.6 %all-gather.46.cloned.1.call-start = ((), (), s32[]{:S(2)}) async-start(), calls=%async_computation.40 | async-start | bytes 4718592 | tf_op jit(solution)/shard_map/all_gather | solution.py:28
  15.0 133.1 %all-gather.44.cloned.1.call-start = ((), (), s32[]{:S(2)}) async-start(), calls=%async_computation.39 | async-start | bytes 7077888 | tf_op jit(solution)/shard_map/all_gather | solution.py:28
  17.2 160.7 %all-gather.32.cloned.1.call-start = ((), (), s32[]{:S(2)}) async-start(), calls=%async_computation.31 | async-start | bytes 2621440 | tf_op jit(solution)/shard_map/all_gather | solution.py:33
  17.8 212.4 %all-gather.42.cloned.1.call-start = ((), (), s32[]{:S(2)}) async-start(), calls=%async_computation.38 | async-start | bytes 9437184 | tf_op jit(solution)/shard_map/all_gather | solution.py:28
  20.2 272.1 %all-gather.40.cloned.1.call-start = ((), (), s32[]{:S(2)}) async-start(), calls=%async_computation.37 | async-start | bytes 11796480 | tf_op jit(solution)/shard_map/all_gather | solution.py:28
  22.9 299.4 %all-gather.30.cloned.1.call-start = ((), (), s32[]{:S(2)}) async-start(), calls=%async_computation.29 | async-start | bytes 2621440 | tf_op jit(solution)/shard_map/all_gather | solution.py:33
  23.7 369.5 %all-gather.38.cloned.1.call-start = ((), (), s32[]{:S(2)}) async-start(), calls=%async_computation.36 | async-start | bytes 14155776 | tf_op jit(solution)/shard_map/all_gather | solution.py:28
  26.5 447.6 %all-gather.36.cloned.1.call-start = ((), (), s32[]{:S(2)}) async-start(), calls=%async_computation.35 | async-start | bytes 16515072 | tf_op jit(solution)/shard_map/all_gather | solution.py:28
  29.5 476.8 %all-gather.28.cloned.1.call-start = ((), (), s32[]{:S(2)}) async-start(), calls=%async_computation.27 | async-start | bytes 2621440 | tf_op jit(solution)/shard_map/all_gather | solution.py:33
  30.3 503.2 %all-gather.26.cloned.1.call-start = ((), (), s32[]{:S(2)}) async-start(), calls=%async_computation.25 | async-start | bytes 2621440 | tf_op jit(solution)/shard_map/all_gather | solution.py:33
  30.9 532.1 %all-gather.24.cloned.1.call-start = ((), (), s32[]{:S(2)}) async-start(), calls=%async_computation.23 | async-start | bytes 2621440 | tf_op jit(solution)/shard_map/all_gather | solution.py:33
  31.7 560.8 %all-gather.22.cloned.1.call-start = ((), (), s32[]{:S(2)}) async-start(), calls=%async_computation.21 | async-start | bytes 2621440 | tf_op jit(solution)/shard_map/all_gather | solution.py:33
  32.4 595.0 %reduce-scatter.41.cloned.1.call-start = ((), (), s32[]{:S(2)}) async-start(), calls=%async_computation.34 | async-start | bytes 4718592 | tf_op jit(solution)/shard_map/reduce_scatter | solution.py:35
  48.1 627.3 %reduce-scatter.27.cloned.1.call-start = ((), (), s32[]{:S(2)}) async-start(), calls=%async_computation.20 | async-start | bytes 5242880 | tf_op jit(solution)/shard_map/reduce_scatter | solution.py:30
  76.2 645.4 %reduce-scatter.25.cloned.1.call-start = ((), (), s32[]{:S(2)}) async-start(), calls=%async_computation.19 | async-start | bytes 5242880 | tf_op jit(solution)/shard_map/reduce_scatter | solution.py:30
  117.8 650.0 %reduce-scatter.23.cloned.1.call-start = ((), (), s32[]{:S(2)}) async-start(), calls=%async_computation.18 | async-start | bytes 5242880 | tf_op jit(solution)/shard_map/reduce_scatter | solution.py:30
  165.4 654.2 %reduce-scatter.39.cloned.1.call-start = ((), (), s32[]{:S(2)}) async-start(), calls=%async_computation.32 | async-start | bytes 9437184 | tf_op jit(solution)/shard_map/reduce_scatter | solution.py:35
  185.5 680.6 %reduce-scatter.21.cloned.1.call-start = ((), (), s32[]{:S(2)}) async-start(), calls=%async_computation.17 | async-start | bytes 5242880 | tf_op jit(solution)/shard_map/reduce_scatter | solution.py:30
  253.0 659.4 %reduce-scatter.19.cloned.1.call-start = ((), (), s32[]{:S(2)}) async-start(), calls=%async_computation.16 | async-start | bytes 5242880 | tf_op jit(solution)/shard_map/reduce_scatter | solution.py:30
  317.7 666.4 %reduce-scatter.37.cloned.1.call-start = ((), (), s32[]{:S(2)}) async-start(), calls=%async_computation.30 | async-start | bytes 14155776 | tf_op jit(solution)/shard_map/reduce_scatter | solution.py:35
  332.3 698.3 %reduce-scatter.17.cloned.1.call-start = ((), (), s32[]{:S(2)}) async-start(), calls=%async_computation.15 | async-start | bytes 5242880 | tf_op jit(solution)/shard_map/reduce_scatter | solution.py:30
  421.8 655.7 %reduce-scatter.15.cloned.1.call-start = ((), (), s32[]{:S(2)}) async-start(), calls=%async_computation.14 | async-start | bytes 5242880 | tf_op jit(solution)/shard_map/reduce_scatter | solution.py:30
  506.2 662.4 %reduce-scatter.35.cloned.1.call-start = ((), (), s32[]{:S(2)}) async-start(), calls=%async_computation.28 | async-start | bytes 18874368 | tf_op jit(solution)/shard_map/reduce_scatter | solution.py:35
  518.9 760.7 %reduce-scatter.33.cloned.1.call-start = ((), (), s32[]{:S(2)}) async-start(), calls=%async_computation.26 | async-start | bytes 23592960 | tf_op jit(solution)/shard_map/reduce_scatter | solution.py:35
  545.7 864.7 %reduce-scatter.31.cloned.1.call-start = ((), (), s32[]{:S(2)}) async-start(), calls=%async_computation.24 | async-start | bytes 28311552 | tf_op jit(solution)/shard_map/reduce_scatter | solution.py:35
  577.2 983.9 %reduce-scatter.29.cloned.1.call-start = ((), (), s32[]{:S(2)}) async-start(), calls=%async_computation.22 | async-start | bytes 33030144 | tf_op jit(solution)/shard_map/reduce_scatter | solution.py:35
  1563.4 1.2 copy-start
  1563.5 1.3 copy-start.1
  1563.5 1.5 copy-start.2
Sparse Core Ops, SparseCore 0:
  11.3 31.7 all-gather.33
  44.6 24.4 all-gather.47
  71.2 33.2 all-gather.45
  106.0 42.0 all-gather.43
  149.5 28.3 all-gather.31
  179.3 50.9 all-gather.41
  231.8 60.4 all-gather.39
  293.9 28.3 all-gather.29
  323.8 69.2 all-gather.37
  395.2 78.8 all-gather.35
  475.6 28.3 all-gather.27
  505.4 27.9 all-gather.25
  535.0 27.9 all-gather.23
  564.5 27.9 all-gather.21
  594.6 32.6 reduce-scatter.40
  629.5 45.8 reduce-scatter.26
  677.6 44.0 reduce-scatter.24
  723.8 44.0 reduce-scatter.22
  770.2 49.3 reduce-scatter.38
  821.7 44.2 reduce-scatter.20
  868.3 43.9 reduce-scatter.18
  914.7 69.3 reduce-scatter.36
  986.4 44.2 reduce-scatter.16
  1033.4 43.9 reduce-scatter.14
  1079.8 88.7 reduce-scatter.34
  1170.8 108.7 reduce-scatter.32
  1281.8 128.5 reduce-scatter.30
  1412.7 148.3 reduce-scatter.28
where the time goes:
time: 1590 us; the launch traced here: 1580 us
  waiting for transfers between devices  1280 us (81%)
  matrix products  145 us (9%)
  local copies, waits for them, and re-layouts  106 us (7%)
  other arithmetic  30.1 us (2%)
    reduce_scatter x7, waiting for transfers between devices, per_device(): lax.psum_scatter(lower_part.reshape(left_rows, col_step, mesh_cols * BLOC...  610 us
    reduce_scatter x7, waiting for transfers between devices, per_device(): lax.psum_scatter(right_part.reshape(row_step, mesh_rows * BLOCK_SIZE, num...  316 us
    all_gather x7, waiting for transfers between devices, per_device(): lax.all_gather(lower_panel.reshape(left_rows, col_step, BLOCK_SIZE), 'col...  276 us
    dot_general x7, matrix products, per_device(): jnp.einsum('rf,bqef->rbqe', grad_rows, side_rows, preferred_element_type=...  77.5 us
    all_gather x7, waiting for transfers between devices, per_device(): lax.all_gather(side_block, 'row', axis=1)  73.8 us
    dot_general x7, matrix products, per_device(): jnp.einsum('rbqe,rf->bqef', gathered, grad_rows, preferred_element_type=j...  67.1 us
    another operation x6, local copies, waits for them, and re-layouts  60.4 us
  transfers between devices with their start and end apart: 28, of which 27 were waited for; matrix products, arithmetic and copies ran while one was open for 17% of the time, Pallas kernels for 0%

commit v1 on v0

v1 whole, which is shorter than its diff:
```python
import functools

import jax
import jax.numpy as jnp
from jax import lax
from jax.experimental import pallas as pl
from jax.experimental.pallas import tpu as pltpu
from jax.sharding import PartitionSpec as P

BLK = 256
NSUM = 2
BF = jnp.bfloat16
F32 = jnp.float32

SLOTS = 57
DX_EVENTS = (5, 9, 13, 17, 22, 26)
LOAD_X = (0, 2, 10, 12, 18, 20, 27, 29)
SUM_X = (1, 3, 11, 13, 19, 21, 28, 30)
SUM_LAG = 4
B_X = (0, 0, 2, 5, 9, 13, 17)
B_START, B_NUM, B_DEN, B_LAG, B_CUT = 3, 3, 4, 3, 4
L_START, L_STRIDE, L_LAG, L_CUT = 3, 3, 3, 3
Y_EVENTS = (6, 12, 18, 24, 28)
T2_A, T2_B = 33, 47
T3_A, T3_NUM, T3_DEN = 31, 8, 7


def _kernel(nr, nc, l_ref, b_ref, x_ref, db_ref, dl_ref, dxg, bc, dxt, ltg, prm, prp,
            lt_in, ltv, dxv, pv, rbm, rbp, sv, dxtv, ltb, acc2, o2, dt, bv, acc3, o3, zero,
            dxs, dxr, bxs, bxr, bys, byr, dys, dyr, lys, lts, ltr, prs, prr, dbs, dbr,
            s_lin, s_dxv, s_rb, s_dxt, s_ltb, s_o2, s_dt, s_bv, s_o3, s_zero, s_own):
    rows, cols = l_ref.shape
    width = x_ref.shape[1]
    ch = 2 * BLK
    nq = rows // ch
    nb = cols // BLK
    tail = [(b, q) for b in range(NSUM, nb) for q in range(b, nq)]
    head = [(b, q) for b in range(NSUM) for q in range(b, nq)]
    nt = len(tail)
    off = {}
    for n, (b, q) in enumerate(tail + head):
        off.setdefault(b, n)
    half = rows // 2
    yrow0 = NSUM * ch
    yhalf = (rows - yrow0) // 2
    per_cut = nt // L_CUT

    z = lax.axis_index("batch")
    r = lax.axis_index("row")
    c = lax.axis_index("col")

    def dev(row, col):
        return (z, row, col)

    def remote(src, dst, ss, rs, to):
        return pltpu.make_async_remote_copy(src, dst, ss, rs, device_id=to, device_id_type=pl.DeviceIdType.MESH)

    def arrived(dst, sem):
        pltpu.make_async_copy(dst, dst, sem).wait()

    def mod(v, m):
        return lax.rem(v + 4 * m, m)

    par = lax.rem(c, 2)
    eps = 1 - 2 * par
    sib = c + eps
    far = mod(c + 4, nc)
    first = mod(c - 2 * eps, nc)
    second = mod(c + 2 * eps, nc)
    hf = par
    hs = 1 - par
    t = lax.rem(c, nr)
    sg = 1 - 2 * lax.rem(t, 2)
    d = mod((r - t) * sg, nr)
    is_root = d == 0
    qc = c // nr

    def row_of(dd):
        return mod(t + sg * dd, nr)

    def piece(o):
        vals = (0, 1, -2, 3, 2, -1, 4, 5)
        v = jnp.int32(vals[0])
        for i in range(1, 8):
            v = jnp.where(o == i, vals[i], v)
        return mod(c + eps * v, nc)

    def block_of(n, order):
        b = jnp.int32(order[0][0])
        st = jnp.int32(0)
        seen = order[0][0]
        for i, (bb, _) in enumerate(order):
            if bb != seen:
                b = jnp.where(n >= i, bb, b)
                st = jnp.where(n >= i, i, st)
                seen = bb
        return b, n - st + b

    bar = pltpu.get_barrier_semaphore()
    for k in range(1, nc):
        pl.semaphore_signal(bar, inc=1, device_id=dev(r, mod(c + k, nc)), device_id_type=pl.DeviceIdType.MESH)
    for k in range(1, nr):
        pl.semaphore_signal(bar, inc=1, device_id=dev(mod(r + k, nr), c), device_id_type=pl.DeviceIdType.MESH)
    pl.semaphore_wait(bar, nc + nr - 2)

    sends = []

    def note(cond, make, grid=None):
        sends.append((cond, make, grid))

    def bx(b, q):
        src = b_ref.at[pl.ds((2 * b + q) * BLK, BLK)]
        return remote(src, bc.at[b, c], bxs.at[b, q], bxr.at[b, c], dev(r, r + nr * q))

    def bx_start(b):
        for q in range(2):
            @pl.when(c != r + nr * q)
            def _():
                bx(b, q).start()

    for b in range(nb):
        for q in range(2):
            note(c != r + nr * q, functools.partial(bx, b, q))

    def dx_own(h, to, i):
        src = x_ref.at[pl.ds(h * half, half)]
        return remote(src, dxg.at[c, pl.ds(h * half, half)], dxs.at[i], dxr.at[c, h], dev(r, to))

    def dx_fwd(p, h, to, i):
        ref = dxg.at[p, pl.ds(h * half, half)]
        return remote(ref, ref, dxs.at[i], dxr.at[p, h], dev(r, to))

    def dx_wait(p, h):
        arrived(dxg.at[p, pl.ds(h * half, half)], dxr.at[p, h])

    own_list = [functools.partial(dx_own, hf, second, 0), functools.partial(dx_own, hs, first, 2),
                functools.partial(dx_own, hf, sib, 4), functools.partial(dx_own, hs, sib, 5),
                functools.partial(dx_own, hs, second, 1), functools.partial(dx_own, hf, first, 3)]
    ev = [(first, hf, [functools.partial(dx_fwd, first, hf, second, 6), functools.partial(dx_fwd, first, hf, sib, 7)]),
          (first, hs, [functools.partial(dx_fwd, first, hs, sib, 8)]),
          (second, hs, [functools.partial(dx_fwd, second, hs, first, 9), functools.partial(dx_fwd, second, hs, sib, 10)]),
          (second, hf, [functools.partial(dx_fwd, second, hf, sib, 11)]),
          (far, hf, [functools.partial(dx_fwd, far, hf, sib, 12)]),
          (far, hs, [functools.partial(dx_fwd, far, hs, sib, 13)])]
    for m in own_list:
        note(None, m)
    for _, _, ms in ev:
        for m in ms:
            note(None, m)

    up = mod(r + 1, nr)
    down = mod(r + nr - 1, nr)
    opp = mod(r + 2, nr)

    def dy_own(h, to, i):
        src = x_ref.at[pl.ds(yrow0 + h * yhalf, yhalf)]
        return remote(src, dxt.at[r, pl.ds(h * yhalf, yhalf)], dys.at[i], dyr.at[r, h], dev(to, c))

    def dy_fwd(p, h, to, i):
        ref = dxt.at[p, pl.ds(h * yhalf, yhalf)]
        return remote(ref, ref, dys.at[i], dyr.at[p, h], dev(to, c))

    def dy_wait(p, h):
        arrived(dxt.at[p, pl.ds(h * yhalf, yhalf)], dyr.at[p, h])

    dy_list = [functools.partial(dy_own, 0, up, 0), functools.partial(dy_own, 1, down, 1),
               functools.partial(dy_own, 1, up, 2), functools.partial(dy_own, 0, down, 3),
               functools.partial(dy_fwd, down, 0, up, 4), functools.partial(dy_fwd, up, 1, down, 5)]
    for m in dy_list:
        note(None, m)

    bx_start(0)
    bx_start(1)
    for m in own_list:
        m().start()
    dy_list[0]().start()
    dy_list[1]().start()

    def load_x(o, slot):
        return pltpu.make_async_copy(x_ref, dxv.at[slot], s_dxv.at[slot])

    load_x(0, 0).start()

    def own_b(b):
        return pltpu.make_async_copy(b_ref.at[pl.ds((2 * b + qc) * BLK, BLK)], sv.at[b, pl.ds(0, BLK)], s_own.at[b])

    def own_b_out(b):
        return pltpu.make_async_copy(sv.at[b, pl.ds(0, BLK)], bc.at[b, c], bxr.at[b, c])

    @pl.when(is_root)
    def _():
        for b in range(nb):
            own_b(b).start()

    zero[...] = jnp.zeros_like(zero)
    zeros = [(b, q) for b in range(nb) for q in range(b)]

    def zero_copy(i):
        b, q = zeros[i]
        return pltpu.make_async_copy(zero, dl_ref.at[pl.ds(q * ch, ch), pl.ds(b * BLK, BLK)], s_zero.at[i])

    for i in range(len(zeros)):
        zero_copy(i).start()

    order = tail + head
    ntot = len(order)

    def lin(n):
        b, q = block_of(n, order)
        src = l_ref.at[pl.ds(pl.multiple_of(q * ch, ch), ch), pl.ds(pl.multiple_of(b * BLK, BLK), BLK)]
        return pltpu.make_async_copy(src, lt_in.at[lax.rem(n, 2)], s_lin.at[lax.rem(n, 2)])

    def ly(i):
        return remote(ltv.at[pl.ds(i * per_cut, per_cut)], ltg.at[qc, r, pl.ds(i * per_cut, per_cut)],
                      lys.at[i], ltr.at[qc, r, i], dev(t, c))

    def l_own(i):
        return pltpu.make_async_copy(ltv.at[pl.ds(i * per_cut, per_cut)], ltg.at[qc, r, pl.ds(i * per_cut, per_cut)],
                                     ltr.at[qc, r, i])

    for i in range(L_CUT):
        note(d != 0, functools.partial(ly, i))

    lin(0).start()

    @pl.loop(0, ntot)
    def _(n):
        lin(n).wait()

        @pl.when(n + 1 < ntot)
        def _():
            lin(n + 1).start()

        ltv[n] = lt_in[lax.rem(n, 2)].T
        for i in range(L_CUT):
            @pl.when(n == (i + 1) * per_cut - 1)
            def _():
                @pl.when(is_root)
                def _():
                    l_own(i).start()

                @pl.when(d != 0)
                def _():
                    ly(i).start()

    @pl.when(is_root)
    def _():
        for b in range(nb):
            own_b(b).wait()
        for b in range(nb):
            own_b_out(b).start()

    on_ring = par == lax.rem(r, 2)

    def l_send(q, e, w, to):
        rr = mod(r + lax.rem(e, nr), nr)
        i = e // nr
        ref = ltg.at[q, rr, pl.ds(i * per_cut, per_cut)]
        return remote(ref, ref, lts.at[e, q, w], ltr.at[q, rr, i], dev(r, to))

    def l_wait(q, e):
        rr = mod(r + lax.rem(e, nr), nr)
        i = e // nr
        arrived(ltg.at[q, rr, pl.ds(i * per_cut, per_cut)], ltr.at[q, rr, i])

    right = mod(c + 2, nc)
    left = mod(c - 2, nc)
    ne = nr * L_CUT

    def l_fwd(q, e):
        side = lax.rem(e, nr) // 2
        from_left = c == mod(r + nr * q + 2, nc)
        cond = jnp.logical_and(jnp.logical_and(on_ring, jnp.logical_not(is_root)), from_left == (side == 0))
        return cond, l_send(q, e, 0, jnp.where(from_left, right, left))

    def l_stage0(e):
        l_wait(qc, e)
        l_send(qc, e, 0, right).start()
        l_send(qc, e, 1, left).start()
        l_send(qc, e, 2, sib).start()

    def l_stage1(e):
        for q in range(2):
            l_wait(q, e)
            cond, cp = l_fwd(q, e)

            @pl.when(cond)
            def _():
                cp.start()
            l_send(q, e, 2, sib).start()

    def l_stage2(e):
        l_wait(1 - qc, e)
        l_send(1 - qc, e, 2, sib).start()

    def l_stage3(e):
        for q in range(2):
            l_wait(q, e)

    bh = BLK // B_CUT
    nv = nb * B_CUT

    def b_ref_of(v, lo, hi):
        return bc.at[v // B_CUT, pl.ds(lo, hi - lo), pl.ds(lax.rem(v, B_CUT) * bh, bh)]

    def b_send(v, lo, hi, ss, rs, dd):
        ref = b_ref_of(v, lo, hi)
        return remote(ref, ref, bys.at[v, ss], byr.at[v, rs], dev(row_of(dd), c))

    def b_wait(v, lo, hi, rs):
        arrived(b_ref_of(v, lo, hi), byr.at[v, rs])

    ja, jc = 3, 6
    b_moves = [(0, lambda v: b_send(v, 0, nc, 0, 0, 3)), (0, lambda v: b_send(v, ja, nc, 1, 0, 1)),
               (3, lambda v: b_send(v, 0, jc, 0, 0, 2)), (1, lambda v: b_send(v, jc, nc, 0, 1, 2)),
               (2, lambda v: b_send(v, 0, ja, 0, 1, 1))]

    def b_active(s):
        def count(x):
            return jnp.clip((x * B_NUM) // B_DEN + 1, 0, nv)
        lo = jnp.where(s > 0, count(s - 1), 0)
        lo = jnp.where(s <= 0, 0, lo)
        hi = jnp.where(s >= 0, count(s), 0)
        return hi > lo, lo

    mrow = ch // 4
    part_rows = ((mrow, ch - mrow), (0, mrow))

    def sum_send(o, part):
        lo, n = part_rows[part]
        to = row_of(mod(d - 1, nr)) if part == 0 else row_of(mod(d + 1, nr))
        dst = (prm if part == 0 else prp).at[o]
        return remote(pv.at[o, pl.ds(lo, n)], dst, prs.at[o, part], prr.at[o, part], dev(to, c))

    def sum_step(o, part, depth):
        lo, n = part_rows[part]
        land = (prm if part == 0 else prp).at[o]
        buf = rbm if part == 0 else rbp

        @pl.when(depth > 0)
        def _():
            arrived(land, prr.at[o, part])
            cp = pltpu.make_async_copy(land, buf, s_rb.at[part])
            cp.start()
            cp.wait()

            @pl.loop(0, n // 64)
            def _(i):
                pv[o, pl.ds(lo + i * 64, 64)] = pv[o, pl.ds(lo + i * 64, 64)] + buf[pl.ds(i * 64, 64)]

        @pl.when(jnp.logical_not(is_root))
        def _():
            sum_send(o, part).start()

    def out_send(o, b, to):
        dst = db_ref.at[pl.ds((2 * b + qc) * BLK, BLK)]
        return remote(sv.at[o, pl.ds(b * BLK, BLK)], dst, dbs.at[o, b], dbr.at[2 * b + qc], dev(r, to))

    def out_local(o, b):
        dst = db_ref.at[pl.ds((2 * b + qc) * BLK, BLK)]
        return pltpu.make_async_copy(sv.at[o, pl.ds(b * BLK, BLK)], dst, dbr.at[2 * b + qc])

    def finish(o):
        @pl.loop(0, ch // 64)
        def _(i):
            sv[o, pl.ds(i * 64, 64)] = pv[o, pl.ds(i * 64, 64)].astype(BF)

        for b in range(NSUM):
            @pl.when(o == 0)
            def _():
                out_local(o, b).start()

            @pl.when(o != 0)
            def _():
                out_send(o, b, piece(o)).start()

    def sum_index(s):
        act = s == SUM_X[0]
        o = jnp.int32(0)
        for i in range(1, 8):
            hit = s == SUM_X[i]
            act = jnp.logical_or(act, hit)
            o = jnp.where(hit, i, o)
        return act, o

    def partial(o):
        slot = lax.rem(o, 2)
        for b in range(NSUM):
            @pl.loop(b, nq)
            def _(q):
                v = jnp.dot(ltv[off[b] + q - b], dxv[slot, pl.ds(pl.multiple_of(q * ch, ch), ch)], preferred_element_type=F32)

                @pl.when(q == b)
                def _():
                    pv[o, pl.ds(b * BLK, BLK)] = v

                @pl.when(q != b)
                def _():
                    pv[o, pl.ds(b * BLK, BLK)] = pv[o, pl.ds(b * BLK, BLK)] + v

    def t2_of(w):
        g = w // nr
        b = NSUM + g // 2
        st = jnp.int32(off[NSUM])
        for bb in range(NSUM + 1, nb):
            st = jnp.where(b == bb, off[bb], st)
        return b, lax.rem(g, 2), lax.rem(w, nr), st

    n2 = (nb - NSUM) * 2 * nr

    def t2_load(w, i):
        b, q, rr, st = t2_of(w)
        k = lax.rem(w, 2)
        return pltpu.make_async_copy(ltg.at[q, rr, st + i], ltb.at[k, i], s_ltb.at[k, i])

    def t2_start(w):
        b = t2_of(w)[0]

        @pl.loop(0, nq - b)
        def _(i):
            t2_load(w, i).start()

    def t2_out(g):
        b, q = NSUM + g // 2, lax.rem(g, 2)
        k = lax.rem(g, 2)
        return pltpu.make_async_copy(o2.at[k], db_ref.at[pl.ds((2 * b + q) * BLK, BLK)], s_o2.at[k])

    def t2_item(w):
        b, q, rr, _ = t2_of(w)
        k = lax.rem(w, 2)
        g = w // nr

        @pl.loop(0, nq - b)
        def _(i):
            t2_load(w, i).wait()

        @pl.when(w + 1 < n2)
        def _():
            t2_start(w + 1)

        @pl.loop(0, nq - b)
        def _(i):
            v = jnp.dot(ltb[k, i], dxtv[rr, pl.ds(pl.multiple_of((b + i - NSUM) * ch, ch), ch)], preferred_element_type=F32)
            fresh = jnp.logical_and(rr == 0, i == 0)

            @pl.when(fresh)
            def _():
                acc2[...] = v

            @pl.when(jnp.logical_not(fresh))
            def _():
                acc2[...] = acc2[...] + v

        @pl.when(rr == nr - 1)
        def _():
            @pl.when(g >= 2)
            def _():
                t2_out(g - 2).wait()
            o2[lax.rem(g, 2)] = acc2[...].astype(BF)
            t2_out(g).start()

    t3_order = [(b, q) for b in range(nb) for q in range(b, nq)]
    n3 = len(t3_order)
    t3_last = [max(n for n, (bb, _) in enumerate(t3_order) if bb == b) for b in range(nb)]

    def t3_load(n, o):
        b, q = block_of(n, t3_order)
        k = lax.rem(n, 2)
        rws = pl.ds(pl.multiple_of(q * ch, ch), ch)
        src = x_ref.at[rws] if o == 0 else dxg.at[mod(c + o, nc), rws]
        return pltpu.make_async_copy(src, dt.at[k, o], s_dt.at[k, o])

    def bv_load(b):
        return pltpu.make_async_copy(bc.at[b], bv.at[lax.rem(b, 2)], s_bv.at[lax.rem(b, 2)])

    def t3_out(n):
        b, q = block_of(n, t3_order)
        k = lax.rem(n, 2)
        dst = dl_ref.at[pl.ds(pl.multiple_of(q * ch, ch), ch), pl.ds(pl.multiple_of(b * BLK, BLK), BLK)]
        return pltpu.make_async_copy(o3.at[k], dst, s_o3.at[k])

    def t3_item(n):
        b, q = block_of(n, t3_order)
        k = lax.rem(n, 2)
        for o in range(nc):
            t3_load(n, o).wait()

        @pl.when(n + 1 < n3)
        def _():
            for o in range(nc):
                t3_load(n + 1, o).start()

        @pl.when(q == b)
        def _():
            bv_load(b).wait()

        @pl.loop(0, nc)
        def _(o):
            v = lax.dot_general(dt[k, o], bv[lax.rem(b, 2), mod(c + o, nc)], (((1,), (1,)), ((), ())), preferred_element_type=F32)

            @pl.when(o == 0)
            def _():
                acc3[...] = v

            @pl.when(o != 0)
            def _():
                acc3[...] = acc3[...] + v

        @pl.when(n >= 2)
        def _():
            t3_out(n - 2).wait()

        for i in range(ch // 128):
            pos = lax.broadcasted_iota(jnp.int32, (128, BLK), 0) + i * 128
            kpos = lax.broadcasted_iota(jnp.int32, (128, BLK), 1)
            rg = ((2 * q + i * 128 // BLK) * nr + r) * BLK + pos % BLK
            cg = (b * nc + c) * BLK + kpos
            o3[k, pl.ds(i * 128, 128)] = jnp.where(rg >= cg, acc3[pl.ds(i * 128, 128)], 0.0).astype(BF)
        t3_out(n).start()
        for b2 in range(nb - 2):
            @pl.when(n == t3_last[b2])
            def _():
                bv_load(b2 + 2).start()

    def t3_count(s):
        return jnp.where(s < T3_A, 0, jnp.clip(((s - T3_A) * T3_NUM) // T3_DEN + 1, 0, n3))

    def t2_count(s):
        first_part = 4 * 2 * 2
        return jnp.clip(s - T2_A + 1, 0, first_part) + jnp.clip((s - T2_B + 1) * 4, 0, n2 - first_part)

    def b_slot(v):
        return B_START + min(x for x in range(200) if (x * B_NUM) // B_DEN + 1 > v)

    def t3_slot(n):
        return T3_A + min(x for x in range(200) if (x * T3_NUM) // T3_DEN + 1 > n)

    for b in range(nb):
        ready = b_slot(B_CUT * b + B_CUT - 1) + 3 * B_LAG
        n0 = 0 if b < 2 else t3_last[b - 2]
        assert t3_slot(n0) >= ready, (b, ready, t3_slot(n0))
    assert T3_A > LOAD_X[7] and T3_A - 1 >= LOAD_X[7]
    assert L_START + L_STRIDE * (2 * nr - 1) + 3 * L_LAG < T2_A + 7 and L_START + L_STRIDE * (ne - 1) + 3 * L_LAG < T2_B
    assert t3_slot(n3 - 1) < SLOTS and T2_B + 6 <= SLOTS and SUM_X[7] + 3 * SUM_LAG < SLOTS

    @pl.loop(0, SLOTS)
    def _(s):
        for i, (p, h, ms) in enumerate(ev):
            @pl.when(s == DX_EVENTS[i])
            def _():
                dx_wait(p, h)
                for m in ms:
                    m().start()

        def l_at(stage, fn, cond):
            x = s - L_START - L_LAG * stage
            act = jnp.logical_and(jnp.logical_and(x >= 0, x < ne * L_STRIDE), lax.rem(jnp.maximum(x, 0), L_STRIDE) == 0)

            @pl.when(jnp.logical_and(act, cond))
            def _():
                fn(x // L_STRIDE)

        l_at(0, l_stage0, is_root)
        l_at(1, l_stage1, jnp.logical_and(on_ring, jnp.logical_not(is_root)))
        l_at(2, l_stage2, is_root)
        l_at(3, l_stage3, jnp.logical_not(on_ring))

        act, v = b_active(s - B_START)

        @pl.when(jnp.logical_and(act, is_root))
        def _():
            @pl.when(lax.rem(v, B_CUT) == 0)
            def _():
                @pl.loop(0, nc)
                def _(j):
                    arrived(bc.at[v // B_CUT, j], bxr.at[v // B_CUT, j])
            b_moves[0][1](v).start()
            b_moves[1][1](v).start()

        act1, v1 = b_active(s - B_START - B_LAG)

        @pl.when(jnp.logical_and(act1, d == 3))
        def _():
            b_wait(v1, 0, nc, 0)
            b_moves[2][1](v1).start()

        @pl.when(jnp.logical_and(act1, d == 1))
        def _():
            b_wait(v1, ja, nc, 0)
            b_moves[3][1](v1).start()

        act2, v2 = b_active(s - B_START - 2 * B_LAG)

        @pl.when(jnp.logical_and(act2, d == 2))
        def _():
            b_wait(v2, 0, jc, 0)
            b_moves[4][1](v2).start()
            b_wait(v2, jc, nc, 1)

        act3, v3 = b_active(s - B_START - 3 * B_LAG)

        @pl.when(jnp.logical_and(act3, d == 1))
        def _():
            b_wait(v3, 0, ja, 1)

        for b in range(2, nb):
            @pl.when(s == B_X[b])
            def _():
                bx_start(b)

        @pl.when(s == Y_EVENTS[0])
        def _():
            dy_list[2]().start()
            dy_list[3]().start()

        @pl.when(s == Y_EVENTS[1])
        def _():
            dy_wait(down, 0)
            dy_list[4]().start()
            dy_wait(up, 1)
            dy_list[5]().start()

        @pl.when(s == Y_EVENTS[2])
        def _():
            dy_wait(down, 1)
            dy_wait(up, 0)

        @pl.when(s == Y_EVENTS[3])
        def _():
            dy_wait(opp, 0)
            dy_wait(opp, 1)

        @pl.when(s == Y_EVENTS[4])
        def _():
            pltpu.make_async_copy(x_ref.at[pl.ds(yrow0, 2 * yhalf)], dxtv.at[r], s_dxt.at[0]).start()
            for i in range(1, nr):
                rr = mod(r + i, nr)
                pltpu.make_async_copy(dxt.at[rr], dxtv.at[rr], s_dxt.at[i]).start()

        for part, depth in ((0, 3 - d), (1, mod(d - 1, nr))):
            sact, o = sum_index(s - SUM_LAG * depth)

            @pl.when(jnp.logical_and(sact, depth > 0))
            def _():
                sum_step(o, part, depth)

        fact, fo = sum_index(s - SUM_LAG * 3)

        @pl.when(jnp.logical_and(fact, is_root))
        def _():
            finish(fo)

        for o in range(1, 8):
            @pl.when(s == LOAD_X[o])
            def _():
                p = piece(o)
                if o % 2 == 1:
                    dx_wait(p, 0)
                    dx_wait(p, 1)
                pltpu.make_async_copy(dxg.at[p], dxv.at[o % 2], s_dxv.at[o % 2]).start()

        pact, po = sum_index(s)

        @pl.when(pact)
        def _():
            load_x(0, lax.rem(po, 2)).wait()
            partial(po)
            for part, depth in ((0, 3 - d), (1, mod(d - 1, nr))):
                @pl.when(depth == 0)
                def _():
                    sum_send(po, part).start()

        @pl.when(s == T2_A - 1)
        def _():
            t2_start(0)
            for i in range(nr):
                pltpu.make_async_copy(x_ref.at[pl.ds(yrow0, 2 * yhalf)], dxtv.at[r], s_dxt.at[i]).wait()

        @pl.when(s == T3_A - 1)
        def _():
            bv_load(0).start()
            bv_load(1).start()
            for o in range(nc):
                t3_load(0, o).start()

        @pl.loop(t2_count(s - 1), t2_count(s))
        def _(w):
            t2_item(w)

        @pl.loop(t3_count(s - 1), t3_count(s))
        def _(n):
            t3_item(n)

    for g in (n2 // nr - 2, n2 // nr - 1):
        t2_out(g).wait()
    for n in (n3 - 2, n3 - 1):
        t3_out(n).wait()
    for i in range(len(zeros)):
        zero_copy(i).wait()
    for i in range(2 * NSUM):
        arrived(db_ref.at[pl.ds(i * BLK, BLK)], dbr.at[i])

    for cond, make, _ in sends:
        if cond is None:
            make().wait_send()
        else:
            @pl.when(cond)
            def _():
                make().wait_send()

    @pl.loop(0, nv)
    def _(v):
        for dd, make in b_moves:
            @pl.when(d == dd)
            def _():
                make(v).wait_send()

    @pl.loop(0, ne)
    def _(e):
        @pl.when(is_root)
        def _():
            l_send(qc, e, 0, right).wait_send()
            l_send(qc, e, 1, left).wait_send()
            l_send(qc, e, 2, sib).wait_send()
            l_send(1 - qc, e, 2, sib).wait_send()

        @pl.when(jnp.logical_and(on_ring, jnp.logical_not(is_root)))
        def _():
            for q in range(2):
                cond, cp = l_fwd(q, e)

                @pl.when(cond)
                def _():
                    cp.wait_send()
                l_send(q, e, 2, sib).wait_send()

    @pl.loop(0, 8)
    def _(o):
        @pl.when(jnp.logical_not(is_root))
        def _():
            for part in range(2):
                sum_send(o, part).wait_send()

        @pl.when(jnp.logical_and(is_root, o != 0))
        def _():
            for b in range(NSUM):
                out_send(o, b, piece(o)).wait_send()


def solution(mesh):
    nr = mesh.shape["row"]
    nc = mesh.shape["col"]
    spec = P(("batch", "row"), "col")

    def per_device(lower_tri, right_side, grad_out):
        rows, cols = lower_tri.shape
        width = right_side.shape[1]
        ch = 2 * BLK
        nq, nb = rows // ch, cols // BLK
        nt = sum(nq - b for b in range(NSUM, nb))
        ntot = sum(nq - b for b in range(nb))
        yrows = rows - NSUM * ch
        nzero = nb * (nb - 1) // 2
        sd = jax.ShapeDtypeStruct
        outs = (sd((rows, width), BF), sd((rows, cols), BF), sd((nc, rows, width), BF), sd((nb, nc, BLK, width), BF),
                sd((nr, yrows, width), BF), sd((2, nr, nt, BLK, ch), BF),
                sd((8, ch - ch // 4, width), F32), sd((8, ch // 4, width), F32))
        vm = pltpu.VMEM
        dma = pltpu.SemaphoreType.DMA
        scratch = [vm((2, ch, BLK), BF), vm((ntot, BLK, ch), BF), vm((2, rows, width), BF), vm((8, ch, width), F32),
                   vm((ch - ch // 4, width), F32), vm((ch // 4, width), F32), vm((8, ch, width), BF),
                   vm((nr, yrows, width), BF), vm((2, nq - NSUM, BLK, ch), BF), vm((BLK, width), F32), vm((2, BLK, width), BF),
                   vm((2, nc, ch, width), BF), vm((2, nc, BLK, width), BF), vm((ch, BLK), F32), vm((2, ch, BLK), BF),
                   vm((ch, BLK), BF),
                   dma((14,)), dma((nc, 2)), dma((nb, 2)), dma((nb, nc)), dma((nb * B_CUT, 2)), dma((nb * B_CUT, 2)),
                   dma((6,)), dma((nr, 2)), dma((L_CUT,)), dma((nr * L_CUT, 2, 3)), dma((2, nr, L_CUT)),
                   dma((8, 2)), dma((8, 2)), dma((8, NSUM)), dma((2 * NSUM,)),
                   dma((2,)), dma((2,)), dma((2,)), dma((nr,)), dma((2, nq - NSUM)), dma((2,)), dma((2, nc)), dma((2,)),
                   dma((2,)), dma((nzero,)), dma((nb,))]
        res = pl.pallas_call(
            functools.partial(_kernel, nr, nc),
            out_shape=outs,
            in_specs=[pl.BlockSpec(memory_space=pl.ANY)] * 3,
            out_specs=tuple(pl.BlockSpec(memory_space=pl.ANY) for _ in outs),
            scratch_shapes=scratch,
            compiler_params=pltpu.CompilerParams(collective_id=0, has_side_effects=True, vmem_limit_bytes=67043328),
            name="tri_backward",
        )(lower_tri, right_side, grad_out)
        return res[0], res[1]

    return jax.shard_map(per_device, mesh=mesh, in_specs=(spec, spec, spec), out_specs=(spec, spec), check_vma=False)
```

time: 1590 us -> 533 us (0.34)
  the two profiles are of different devices: /device:TPU:97 before, /device:TPU:118 now
where the time goes in v1:
time: 533 us; the launch traced here: 531 us
  Pallas kernels  515 us (97%)
  local copies, waits for them, and re-layouts  14.7 us (3%)
    pallas_call x1, Pallas kernels, per_device(): pl.pallas_call(functools.partial(_kernel, nr, nc), out_shape=outs, in_spe...  515 us
    unnamed x2, local copies, waits for them, and re-layouts  14.7 us

profile of v1, /device:TPU:118, one launch (start us, length us, event | category | flops | bytes accessed | tf_op | source)
XLA Modules:
  0.0 530.7 jit_solution(1737192096070431694)
XLA Ops:
  0.6 515.4 %tri_backward.1 = (bf16[3584,512]{1,0:T(8,128)(2,1)}, bf16[3584,1792]{1,0:T(8,128)(2,1)}, bf16[8,3584,512]{2,1,0:T(8,128)(2,1)}, bf16[7,8,256,512]{3,2,1,0:T(8,1...) custom-call(bf16[3584,1792]{1,0:T(8,128)(2,1)} %l_ref.1, ...), custom_call_target="tpu_custom_call" | custom-call | tf_op jit(solution)/shard_map/tri_backward/pallas_call | solution.py:780
  516.0 4.1 copy.7
  520.1 10.6 %copy.8 = bf16[3584,1792]{1,0:T(8,128)(2,1)} copy(bf16[3584,1792]{1,0:T(8,128)(2,1)} %get-tuple-element.9) | data formatting | bytes 25690112

commit v2 on v1

v2 whole, which is shorter than its diff:
```python
import functools

import jax
import jax.numpy as jnp
from jax import lax
from jax.experimental import pallas as pl
from jax.experimental.pallas import tpu as pltpu
from jax.sharding import PartitionSpec as P

BLK = 256
NSUM = 3
BF = jnp.bfloat16
F32 = jnp.float32

B_CUT = 4
L_CUT = 3
L_BUF = 4
DX_SEND = 20
DX_EVENTS = (28, 38, 42, 52, 61, 82)
SUM_X = (7, 9, 43, 47, 55, 57, 88, 97)
SUM_LINES = ((38, 50, 4), (73, 33, 4), (74, 40, 4))
BX_LINE = (9, 37, 4)
B_LINES = ((24, 16, 4), (40, 14, 4), (90, 8, 4), (99, 7, 4))
L_LINES = ((49, 6, 4), (84, 14, 4), (91, 13, 4), (95, 13, 4))
Y_EVENTS = (10, 15, 12, 55, 55, 65, 72)
T2_A = 125
T3_A = 98
PER_SLOT = 2
JA, JC, SUM_UP = 3, 4, 64


def _line(line, n):
    first, num, den = line
    return tuple(first + i * num // den for i in range(n))


def _kernel(nr, nc, l_ref, b_ref, x_ref, db_ref, dl_ref, dxg, bc, dxt, ltg, prm, prp,
            lt_in, ltv, lth, dxv, pv, rbm, rbp, sv, dxtv, ltb, acc2, o2, dt, bv, acc3, o3,
            dxs, dxr, bxs, bxr, bys, byr, dys, dyr, lys, lts, ltr, prs, prr, dbs, dbr,
            s_ltz, s_lin, s_dxv, s_rb, s_dxt, s_ltb, s_o2, s_dt, s_bv, s_o3, s_zero, s_own):
    rows, cols = l_ref.shape
    width = x_ref.shape[1]
    ch = 2 * BLK
    nq = rows // ch
    nb = cols // BLK
    tail = [(b, b) for b in range(NSUM, nb)] + [(b, q) for b in range(NSUM, nb) for q in range(b + 1, nq)]
    ndiag = nb - NSUM
    head = [(b, q) for b in range(NSUM) for q in range(b, nq)]
    nt = len(tail)
    off = {}
    for n, (b, q) in enumerate(tail + head):
        off.setdefault(b, n)
    half = rows // 2
    yrow0 = NSUM * ch
    yhalf = (rows - yrow0) // 2
    cuts = [n for n in range(nt) if n in (0, ndiag) or tail[n - 1][0] != tail[n][0] and n > ndiag][:L_CUT] + [nt]

    nv = nb * B_CUT
    ne = nr * L_CUT
    load_x_at = tuple(max(x - 1, 0) for x in SUM_X)
    sum_at = tuple(_line(x, nc) for x in SUM_LINES)
    bx_at = _line(BX_LINE, nb)
    b_slot = tuple(_line(x, nv) for x in B_LINES)
    l_slot = tuple(_line(x, ne) for x in L_LINES)

    z = lax.axis_index("batch")
    r = lax.axis_index("row")
    c = lax.axis_index("col")

    def dev(row, col):
        return (z, row, col)

    def remote(src, dst, ss, rs, to):
        return pltpu.make_async_remote_copy(src, dst, ss, rs, device_id=to, device_id_type=pl.DeviceIdType.MESH)

    def arrived(dst, sem):
        pltpu.make_async_copy(dst, dst, sem).wait()

    def mod(v, m):
        return lax.rem(v + 4 * m, m)

    par = lax.rem(c, 2)
    eps = 1 - 2 * par
    sib = c + eps
    far = mod(c + 4, nc)
    first = mod(c - 2 * eps, nc)
    second = mod(c + 2 * eps, nc)
    hf = par
    hs = 1 - par
    t = lax.rem(c, nr)
    sg = 1 - 2 * lax.rem(t, 2)
    d = mod((r - t) * sg, nr)
    is_root = d == 0
    qc = c // nr

    def row_of(dd):
        return mod(t + sg * dd, nr)

    def piece(o):
        vals = (0, 1, -2, 3, 2, -1, 4, 5)
        v = jnp.int32(vals[0])
        for i in range(1, 8):
            v = jnp.where(o == i, vals[i], v)
        return mod(c + eps * v, nc)

    def table(n, vals):
        v = jnp.int32(vals[0])
        for i in range(1, len(vals)):
            if vals[i] != vals[i - 1]:
                v = jnp.where(n >= i, vals[i], v)
        return v

    def block_of(n, order):
        return table(n, [b for b, _ in order]), table(n, [q for _, q in order])

    bar = pltpu.get_barrier_semaphore()
    for k in range(1, nc):
        pl.semaphore_signal(bar, inc=1, device_id=dev(r, mod(c + k, nc)), device_id_type=pl.DeviceIdType.MESH)
    for k in range(1, nr):
        pl.semaphore_signal(bar, inc=1, device_id=dev(mod(r + k, nr), c), device_id_type=pl.DeviceIdType.MESH)
    pl.semaphore_wait(bar, nc + nr - 2)

    sends = []

    def note(cond, make, grid=None):
        sends.append((cond, make, grid))

    def bx(b, q):
        src = b_ref.at[pl.ds((2 * b + q) * BLK, BLK)]
        return remote(src, bc.at[b, c], bxs.at[b, q], bxr.at[b, c], dev(r, r + nr * q))

    def bx_start(b):
        for q in range(2):
            @pl.when(c != r + nr * q)
            def _():
                bx(b, q).start()

    for b in range(nb):
        for q in range(2):
            note(c != r + nr * q, functools.partial(bx, b, q))

    def dx_own(h, to, i):
        src = x_ref.at[pl.ds(h * half, half)]
        return remote(src, dxg.at[c, pl.ds(h * half, half)], dxs.at[i], dxr.at[c, h], dev(r, to))

    def dx_fwd(p, h, to, i):
        ref = dxg.at[p, pl.ds(h * half, half)]
        return remote(ref, ref, dxs.at[i], dxr.at[p, h], dev(r, to))

    def dx_wait(p, h):
        arrived(dxg.at[p, pl.ds(h * half, half)], dxr.at[p, h])

    own_list = [functools.partial(dx_own, hf, second, 0), functools.partial(dx_own, hf, sib, 4),
                functools.partial(dx_own, hs, second, 1), functools.partial(dx_own, hs, sib, 5),
                functools.partial(dx_own, hs, first, 2), functools.partial(dx_own, hf, first, 3)]
    ev = [(first, hf, [functools.partial(dx_fwd, first, hf, second, 6), functools.partial(dx_fwd, first, hf, sib, 7)]),
          (first, hs, [functools.partial(dx_fwd, first, hs, sib, 8)]),
          (second, hs, [functools.partial(dx_fwd, second, hs, first, 9), functools.partial(dx_fwd, second, hs, sib, 10)]),
          (second, hf, [functools.partial(dx_fwd, second, hf, sib, 11)]),
          (far, hf, [functools.partial(dx_fwd, far, hf, sib, 12)]),
          (far, hs, [functools.partial(dx_fwd, far, hs, sib, 13)])]
    for m in own_list:
        note(None, m)
    for _, _, ms in ev:
        for m in ms:
            note(None, m)

    up = mod(r + 1, nr)
    down = mod(r + nr - 1, nr)
    opp = mod(r + 2, nr)

    def dy_own(h, to, i):
        src = x_ref.at[pl.ds(yrow0 + h * yhalf, yhalf)]
        return remote(src, dxt.at[r, pl.ds(h * yhalf, yhalf)], dys.at[i], dyr.at[r, h], dev(to, c))

    def dy_fwd(p, h, to, i):
        ref = dxt.at[p, pl.ds(h * yhalf, yhalf)]
        return remote(ref, ref, dys.at[i], dyr.at[p, h], dev(to, c))

    def dy_wait(p, h):
        arrived(dxt.at[p, pl.ds(h * yhalf, yhalf)], dyr.at[p, h])

    dy_list = [functools.partial(dy_own, 0, up, 0), functools.partial(dy_own, 1, down, 1),
               functools.partial(dy_own, 1, up, 2), functools.partial(dy_own, 0, down, 3),
               functools.partial(dy_fwd, down, 0, up, 4), functools.partial(dy_fwd, up, 1, down, 5)]
    for m in dy_list:
        note(None, m)

    own_list[0]().start()
    own_list[1]().start()
    bx_start(0)
    own_list[2]().start()
    own_list[3]().start()
    dy_list[0]().start()
    dy_list[1]().start()

    def load_x(o, slot):
        return pltpu.make_async_copy(x_ref, dxv.at[slot], s_dxv.at[slot])

    load_x(0, 0).start()

    def own_b(b):
        return pltpu.make_async_copy(b_ref.at[pl.ds((2 * b + qc) * BLK, BLK)], sv.at[b, pl.ds(0, BLK)], s_own.at[b])

    def own_b_out(b):
        return pltpu.make_async_copy(sv.at[b, pl.ds(0, BLK)], bc.at[b, c], bxr.at[b, c])

    @pl.when(is_root)
    def _():
        for b in range(nb):
            own_b(b).start()

    zeros = [(b, q) for b in range(nb) for q in range(b)]

    def zero_copy(i):
        b, q = zeros[i]
        return pltpu.make_async_copy(lt_in.at[0], dl_ref.at[pl.ds(q * ch, ch), pl.ds(b * BLK, BLK)], s_zero.at[i])

    order = tail + head
    ntot = len(order)

    def lin(n):
        b, q = block_of(n, order)
        src = l_ref.at[pl.ds(pl.multiple_of(q * ch, ch), ch), pl.ds(pl.multiple_of(b * BLK, BLK), BLK)]
        return pltpu.make_async_copy(src, lt_in.at[lax.rem(n, L_BUF)], s_lin.at[lax.rem(n, L_BUF)])

    def part_of(ref, i, full):
        n = cuts[i + 1] - cuts[i]
        return ref.at[pl.ds(cuts[i], n)] if full else ref.at[pl.ds(cuts[i], n), :, pl.ds(BLK, BLK)]

    def level(home, src_row, q, i):
        return jnp.where(src_row >= home, 2, 1) - q if i == 0 else jnp.int32(2)

    def by_level(i, lvl, fn):
        @pl.when(lvl == 2)
        def _():
            fn(True)

        if i == 0:
            @pl.when(lvl == 1)
            def _():
                fn(False)

    def ly(i, full):
        return remote(part_of(ltv, i, full), part_of(ltg.at[qc, r], i, full), lys.at[i], ltr.at[qc, r, i], dev(t, c))

    def ly_do(i, op):
        @pl.when(d != 0)
        def _():
            by_level(i, level(t, r, qc, i), lambda full: op(ly(i, full)))

    def l_own(i):
        return pltpu.make_async_copy(part_of(ltv, i, True), part_of(ltg.at[qc, r], i, True), ltr.at[qc, r, i])

    def l_zero(q, rr, j):
        src = lt_in.at[pl.ds(0, ndiag), pl.ds(0, BLK)]
        return pltpu.make_async_copy(src, ltg.at[q, rr, pl.ds(0, ndiag), :, pl.ds(j * BLK, BLK)], s_ltz.at[q, rr, j])

    def l_zeros(op):
        @pl.loop(0, nr)
        def _(rr):
            for q in range(2):
                lvl = level(r, rr, q, 0)
                mine = jnp.logical_and(is_root, jnp.logical_and(rr == r, qc == q))
                for j in range(2):
                    @pl.when(jnp.logical_and(lvl < 2 - j, jnp.logical_not(mine)))
                    def _():
                        op(l_zero(q, rr, j))

    for n in range(L_BUF - 1):
        lin(n).start()
    for b in range(1, NSUM):
        lth[pl.ds(b * BLK, BLK), pl.ds(0, b * ch)] = jnp.zeros((BLK, b * ch), BF)

    @pl.loop(0, ntot)
    def _(n):
        lin(n).wait()

        @pl.when(n + L_BUF - 1 < ntot)
        def _():
            lin(n + L_BUF - 1).start()

        blk = lt_in[lax.rem(n, L_BUF)].T

        @pl.when(n < nt)
        def _():
            ltv[n] = blk

        @pl.when(n >= nt)
        def _():
            b, q = block_of(n, order)
            lth[pl.ds(pl.multiple_of(b * BLK, BLK), BLK), pl.ds(pl.multiple_of(q * ch, ch), ch)] = blk

        for i in range(L_CUT):
            @pl.when(n == cuts[i + 1] - 1)
            def _():
                @pl.when(is_root)
                def _():
                    l_own(i).start()

                ly_do(i, lambda cp: cp.start())

    lt_in[...] = jnp.zeros_like(lt_in)
    l_zeros(lambda cp: cp.start())
    for i in range(len(zeros)):
        zero_copy(i).start()

    @pl.when(is_root)
    def _():
        for b in range(nb):
            own_b(b).wait()
        for b in range(nb):
            own_b_out(b).start()

    on_ring = par == lax.rem(r, 2)

    def l_do(q, e, w, to, op):
        rr = mod(r + lax.rem(e, nr), nr)

        def go(i, full):
            ref = part_of(ltg.at[q, rr], i, full)
            op(remote(ref, ref, lts.at[e, q, w], ltr.at[q, rr, i], dev(r, to)))

        for i in range(L_CUT):
            @pl.when(e // nr == i)
            def _():
                by_level(i, level(r, rr, q, i), functools.partial(go, i))

    def l_send(q, e, w, to):
        l_do(q, e, w, to, lambda cp: cp.start())

    def l_wait(q, e):
        rr = mod(r + lax.rem(e, nr), nr)
        mine = jnp.logical_and(is_root, jnp.logical_and(rr == r, qc == q))

        def go(i, full):
            arrived(part_of(ltg.at[q, rr], i, full), ltr.at[q, rr, i])

        for i in range(L_CUT):
            @pl.when(e // nr == i)
            def _():
                by_level(i, jnp.where(mine, 2, level(r, rr, q, i)), functools.partial(go, i))

    right = mod(c + 2, nc)
    left = mod(c - 2, nc)
    def l_fwd(q, e, op):
        side = lax.rem(e, nr) // 2
        from_left = c == mod(r + nr * q + 2, nc)

        @pl.when(from_left == (side == 0))
        def _():
            l_do(q, e, 0, jnp.where(from_left, right, left), op)

    def l_stage0(e):
        l_wait(qc, e)
        l_send(qc, e, 0, right)
        l_send(qc, e, 1, left)
        l_send(qc, e, 2, sib)

    def l_stage1(e):
        for q in range(2):
            l_wait(q, e)
            l_fwd(q, e, lambda cp: cp.start())
            l_send(q, e, 2, sib)

    def l_stage2(e):
        l_wait(1 - qc, e)
        l_send(1 - qc, e, 2, sib)

    def l_stage3(e):
        for q in range(2):
            l_wait(q, e)

    bh = BLK // B_CUT

    def b_ref_of(v, lo, hi):
        return bc.at[v // B_CUT, pl.ds(lo, hi - lo), pl.ds(lax.rem(v, B_CUT) * bh, bh)]

    def b_send(v, lo, hi, ss, rs, dd):
        ref = b_ref_of(v, lo, hi)
        return remote(ref, ref, bys.at[v, ss], byr.at[v, rs], dev(row_of(dd), c))

    def b_wait(v, lo, hi, rs):
        arrived(b_ref_of(v, lo, hi), byr.at[v, rs])

    ja, jc = JA, JC
    b_moves = [(0, lambda v: b_send(v, 0, nc, 0, 0, 3)), (0, lambda v: b_send(v, ja, nc, 1, 0, 1)),
               (3, lambda v: b_send(v, 0, jc, 0, 0, 2)), (1, lambda v: b_send(v, jc, nc, 0, 1, 2)),
               (2, lambda v: b_send(v, 0, ja, 0, 1, 1))]

    mrow = SUM_UP
    prows = NSUM * BLK
    part_rows = ((mrow, prows - mrow), (0, mrow))

    def sum_send(o, part):
        lo, n = part_rows[part]
        to = row_of(mod(d - 1, nr)) if part == 0 else row_of(mod(d + 1, nr))
        dst = (prm if part == 0 else prp).at[o]
        return remote(pv.at[o, pl.ds(lo, n)], dst, prs.at[o, part], prr.at[o, part], dev(to, c))

    def sum_step(o, part, depth):
        lo, n = part_rows[part]
        land = (prm if part == 0 else prp).at[o]
        buf = rbm if part == 0 else rbp

        arrived(land, prr.at[o, part])
        cp = pltpu.make_async_copy(land, buf, s_rb.at[part])
        cp.start()
        cp.wait()

        @pl.loop(0, n // 64)
        def _(i):
            pv[o, pl.ds(lo + i * 64, 64)] = pv[o, pl.ds(lo + i * 64, 64)] + buf[pl.ds(i * 64, 64)]

        @pl.when(jnp.logical_not(is_root))
        def _():
            sum_send(o, part).start()

    def out_send(o, b, to):
        dst = db_ref.at[pl.ds((2 * b + qc) * BLK, BLK)]
        return remote(sv.at[o, pl.ds(b * BLK, BLK)], dst, dbs.at[o, b], dbr.at[2 * b + qc], dev(r, to))

    def out_local(o, b):
        dst = db_ref.at[pl.ds((2 * b + qc) * BLK, BLK)]
        return pltpu.make_async_copy(sv.at[o, pl.ds(b * BLK, BLK)], dst, dbr.at[2 * b + qc])

    def finish(o):
        @pl.loop(0, prows // 64)
        def _(i):
            sv[o, pl.ds(i * 64, 64)] = pv[o, pl.ds(i * 64, 64)].astype(BF)

        for b in range(NSUM):
            @pl.when(o == 0)
            def _():
                out_local(o, b).start()

            @pl.when(o != 0)
            def _():
                out_send(o, b, piece(o)).start()

    def partial(o):
        pv[o] = jnp.dot(lth[...], dxv[lax.rem(o, 2)], preferred_element_type=F32)

    offd = [next((n for n, x in enumerate(tail) if n >= ndiag and x[0] == b), nt) for b in range(NSUM, nb)]
    n2 = (nb - NSUM) * nr

    def t2_load(w, q, i):
        g, k = w // nr, lax.rem(w, 2)
        n = jnp.where(i == 0, g, table(g, offd) + i - 1)
        dst = ltb.at[k, pl.ds(q * BLK, BLK), pl.ds(pl.multiple_of(i * ch, ch), ch)]
        return pltpu.make_async_copy(ltg.at[q, lax.rem(w, nr), n], dst, s_ltb.at[k, q, i])

    def t2_loads(w, op):
        @pl.loop(0, nq - NSUM - w // nr)
        def _(i):
            for q in range(2):
                op(t2_load(w, q, i))

    def t2_start(w):
        t2_loads(w, lambda cp: cp.start())

    def t2_out(g):
        k = lax.rem(g, 2)
        return pltpu.make_async_copy(o2.at[k], db_ref.at[pl.ds((NSUM + g) * ch, ch)], s_o2.at[k])

    def t2_item(w):
        g, rr, k = w // nr, lax.rem(w, nr), lax.rem(w, 2)
        t2_loads(w, lambda cp: cp.wait())

        @pl.when(w + 1 < n2)
        def _():
            t2_start(w + 1)

        for gg in range(nb - NSUM):
            @pl.when(g == gg)
            def _():
                deep = (nq - NSUM - gg) * ch
                v = jnp.dot(ltb[k, :, pl.ds(0, deep)], dxtv[rr, pl.ds(gg * ch, deep)], preferred_element_type=F32)

                @pl.when(rr == 0)
                def _():
                    acc2[...] = v

                @pl.when(rr != 0)
                def _():
                    acc2[...] = acc2[...] + v

        @pl.when(rr == nr - 1)
        def _():
            @pl.when(g >= 2)
            def _():
                t2_out(g - 2).wait()
            o2[lax.rem(g, 2)] = acc2[...].astype(BF)
            t2_out(g).start()

    t3_order = [(b, q) for b in range(nb) for q in range(b, nq)]
    n3 = len(t3_order)
    t3_last = [max(n for n, (bb, _) in enumerate(t3_order) if bb == b) for b in range(nb)]

    def t3_load(n, o):
        b, q = block_of(n, t3_order)
        k = lax.rem(n, 2)
        rws = pl.ds(pl.multiple_of(q * ch, ch), ch)
        src = x_ref.at[rws] if o == 0 else dxg.at[mod(c + o, nc), rws]
        return pltpu.make_async_copy(src, dt.at[k, :, pl.ds(pl.multiple_of(mod(c + o, nc) * width, width), width)], s_dt.at[k, o])

    def bv_load(b, j):
        k = lax.rem(b, 2)
        return pltpu.make_async_copy(bc.at[b, j], bv.at[k, :, pl.ds(j * width, width)], s_bv.at[k, j])

    def t3_out(n):
        b, q = block_of(n, t3_order)
        k = lax.rem(n, 2)
        dst = dl_ref.at[pl.ds(pl.multiple_of(q * ch, ch), ch), pl.ds(pl.multiple_of(b * BLK, BLK), BLK)]
        return pltpu.make_async_copy(o3.at[k], dst, s_o3.at[k])

    def t3_item(n):
        b, q = block_of(n, t3_order)
        k = lax.rem(n, 2)
        for o in range(nc):
            t3_load(n, o).wait()

        @pl.when(n + 1 < n3)
        def _():
            for o in range(nc):
                t3_load(n + 1, o).start()

        @pl.when(q == b)
        def _():
            for j in range(nc):
                bv_load(b, j).wait()

        acc3[...] = lax.dot_general(dt[k], bv[lax.rem(b, 2)], (((1,), (1,)), ((), ())), preferred_element_type=F32)

        @pl.when(n >= 2)
        def _():
            t3_out(n - 2).wait()

        for i in range(ch // 128):
            pos = lax.broadcasted_iota(jnp.int32, (128, BLK), 0) + i * 128
            kpos = lax.broadcasted_iota(jnp.int32, (128, BLK), 1)
            rg = ((2 * q + i * 128 // BLK) * nr + r) * BLK + pos % BLK
            cg = (b * nc + c) * BLK + kpos
            o3[k, pl.ds(i * 128, 128)] = jnp.where(rg >= cg, acc3[pl.ds(i * 128, 128)], 0.0).astype(BF)
        t3_out(n).start()
    b_ready = [max(x[B_CUT * b + B_CUT - 1] for x in b_slot) for b in range(nb)]
    l_ready = [max(x[nr * i + nr - 1] for x in l_slot) for i in range(L_CUT)]
    t2_need = [l_ready[min(w // nr + 1, L_CUT - 1)] for w in range(n2)]

    def b_loads(slots):
        return [max(b_ready[b], T3_A - 1 if b < 2 else slots[t3_last[b - 2]]) for b in range(nb)]

    def earliest(begin, end, n, fits):
        found = []
        for first in range(begin, end):
            num = next((m for m in range(2, BLK) if fits(_line((first, m, 4), n))), None)
            if num is not None:
                found.append((_line((first, num, 4), n)[-1], first, num))
        _, first, num = min(found)
        return first, num, _line((first, num, 4), n)

    t2_first_slot, t2_num, t2_slots = earliest(T2_A, T2_A + 2, n2, lambda x: all(x[w] >= t2_need[min(w + 1, n2 - 1)] for w in range(n2)))
    t3_first_slot, t3_num, t3_slots = earliest(
        max(T3_A, b_ready[0] + 1), max(T3_A, b_ready[1]) + 2, n3,
        lambda x: all(a > y for a, y in zip((x[t3_last[b] + b - nb + 1] for b in range(nb)), b_loads(x))))
    bv_slots = b_loads(t3_slots)
    assert T2_A > max(l_ready[1], Y_EVENTS[6]) and Y_EVENTS[6] > max(Y_EVENTS[3:6])
    assert T3_A > max(load_x_at[-1], DX_EVENTS[-1])
    lists = ((SUM_X,) + sum_at, b_slot, l_slot)
    assert all(a < b for f in lists for x in f for a, b in zip(x[:-1], x[1:]))
    assert all(a < b for f in lists for y, z in zip(f[:-1], f[1:]) for a, b in zip(y, z))
    assert all(SUM_X[o - 2] < load_x_at[o] for o in range(2, nc))
    assert all(max(DX_EVENTS[o:o + 2]) <= load_x_at[o + 2] for o in (0, 2, 4))
    assert all(b_slot[0][B_CUT * b] <= sum_at[-1][b] for b in range(nb))
    slots = 1 + max(t3_slots[-1], t2_slots[-1], sum_at[-1][-1], b_ready[-1], l_ready[-1])

    down_depth = nr - 1 - d
    up_depth = mod(d - 1, nr)
    off_ring = jnp.logical_not(on_ring)

    events = []

    def event(slot, fn):
        events.append((slot, fn))

    def dx_event(i):
        p, h, ms = ev[i]
        dx_wait(p, h)
        for m in ms:
            m().start()

    def dx_rest():
        for m in own_list[4:]:
            m().start()

    def bx_event(b):
        bx_start(b)

    def y_first():
        dy_list[2]().start()
        dy_list[3]().start()

    def y_event(i):
        if i == 1:
            dy_wait(down, 0)
            dy_list[4]().start()
        elif i == 2:
            dy_wait(up, 1)
            dy_list[5]().start()
        elif i == 3:
            dy_wait(down, 1)
        elif i == 4:
            dy_wait(up, 0)
        else:
            dy_wait(opp, 0)
            dy_wait(opp, 1)

    def y_load(op):
        for i in range(nr):
            rr = mod(r + i, nr)
            src = x_ref.at[pl.ds(yrow0, 2 * yhalf)] if i == 0 else dxt.at[rr]
            op(pltpu.make_async_copy(src, dxtv.at[rr], s_dxt.at[i]))

    def t2_first():
        l_zeros(lambda cp: cp.wait())
        t2_start(0)
        y_load(lambda cp: cp.wait())

    def t3_first():
        for o in range(nc):
            t3_load(0, o).start()

    def bv_event(b):
        for j in range(nc):
            bv_load(b, j).start()

    for i in range(len(ev)):
        event(DX_EVENTS[i], functools.partial(dx_event, i))
    event(DX_SEND, dx_rest)
    for b in range(1, nb):
        event(bx_at[b], functools.partial(bx_event, b))
    event(Y_EVENTS[0], y_first)
    for i in range(1, 6):
        event(Y_EVENTS[i], functools.partial(y_event, i))
    event(Y_EVENTS[6], lambda: y_load(lambda cp: cp.start()))
    n_first = len(events)
    event(T2_A - 1, t2_first)
    event(T3_A - 1, t3_first)
    for b in range(nb):
        event(bv_slots[b], functools.partial(bv_event, b))
    masks = {}
    for i, (x, _) in enumerate(events):
        masks[x] = masks.get(x, 0) + (1 << i)

    def mask_of(s):
        m = jnp.int32(0)
        for x in sorted(masks):
            m = jnp.where(s == x, masks[x], m)
        return m

    def run_events(mask, lo, hi):
        part = sum(1 << i for i in range(lo, hi))

        @pl.when(jnp.bitwise_and(mask, part) != 0)
        def _():
            for i in range(lo, hi):
                @pl.when(jnp.bitwise_and(mask, 1 << i) != 0)
                def _():
                    events[i][1]()

    def b_due(v):
        @pl.when(is_root)
        def _():
            @pl.when(lax.rem(v, B_CUT) == 0)
            def _():
                @pl.loop(0, nc)
                def _(j):
                    arrived(bc.at[v // B_CUT, j], bxr.at[v // B_CUT, j])
            b_moves[0][1](v).start()
            b_moves[1][1](v).start()

        @pl.when(d == 3)
        def _():
            b_wait(v, 0, nc, 0)
            b_moves[2][1](v).start()

        @pl.when(d == 1)
        def _():
            b_wait(v, ja, nc, 0)
            b_moves[3][1](v).start()

        @pl.when(d == 2)
        def _():
            b_wait(v, 0, jc, 0)
            b_moves[4][1](v).start()
            b_wait(v, jc, nc, 1)

    def b_last(v):
        b_wait(v, 0, ja, 1)

    def l_due(e):
        @pl.when(is_root)
        def _():
            l_stage0(e)

        @pl.when(off_ring)
        def _():
            l_stage3(e)

        @pl.when(jnp.logical_and(on_ring, jnp.logical_not(is_root)))
        def _():
            l_stage1(e)

    def sum_due(o, part, depth):
        sum_step(o, part, depth)

    def load_due(o):
        p = piece(o)
        k = lax.rem(o, 2)

        @pl.when(k == 1)
        def _():
            dx_wait(p, 0)
            dx_wait(p, 1)

        @pl.when(o > 0)
        def _():
            pltpu.make_async_copy(dxg.at[p], dxv.at[k], s_dxv.at[k]).start()

    def part_due(o):
        load_x(0, lax.rem(o, 2)).wait()
        partial(o)
        for part, depth in ((0, down_depth), (1, up_depth)):
            @pl.when(depth == 0)
            def _():
                sum_send(o, part).start()

    def stage(lines, k):
        first = jnp.int32(slots)
        num = jnp.int32(0)
        for i, (f, m, _) in enumerate(lines):
            first = jnp.where(k == i, f, first)
            num = jnp.where(k == i, m, num)
        return lambda n: first + n * num // 4

    def listed(vals):
        return lambda n: table(n, vals + (slots,))

    def up_due(o):
        sum_due(o, 1, up_depth)

        @pl.when(is_root)
        def _():
            finish(o)

    none = jnp.int32(-1)
    flows = [(stage(L_LINES, jnp.where(is_root, 0, jnp.where(off_ring, 3, 1))), ne, l_due),
             (stage(L_LINES, jnp.where(is_root, 2, none)), ne, l_stage2),
             (stage(B_LINES, jnp.where(d == 0, 0, jnp.where(d == 2, 2, 1))), nv, b_due),
             (stage(B_LINES, jnp.where(d == 1, 3, none)), nv, b_last),
             (stage(SUM_LINES, down_depth - 1), nc, lambda o: sum_due(o, 0, down_depth)),
             (stage(SUM_LINES, up_depth - 1), nc, up_due),
             (listed(load_x_at), nc, load_due),
             (listed(SUM_X), nc, part_due)]
    work = [(lambda n: t2_first_slot + n * t2_num // 4, n2, t2_item), (lambda n: t3_first_slot + n * t3_num // 4, n3, t3_item)]

    def slot(s, carry):
        nxt = list(carry)
        mask = mask_of(s)
        run_events(mask, 0, n_first)

        def due(i, when, total, fn):
            n = nxt[i]
            hit = jnp.logical_and(n < total, when(n) == s)

            @pl.when(hit)
            def _():
                fn(n)

            nxt[i] = jnp.where(hit, n + 1, n)

        for i, (when, total, fn) in enumerate(flows):
            due(i, when, total, fn)
        run_events(mask, n_first, n_first + 2)
        for i, (when, total, fn) in enumerate(work):
            k = len(flows) + i

            def again(_, n):
                hit = jnp.logical_and(n < total, when(n) == s)

                @pl.when(hit)
                def _():
                    fn(n)

                return jnp.where(hit, n + 1, n)

            nxt[k] = lax.fori_loop(0, PER_SLOT, again, nxt[k])
        run_events(mask, n_first + 2, len(events))
        return tuple(nxt)

    lax.fori_loop(0, slots, slot, tuple(jnp.int32(0) for _ in range(len(flows) + len(work))))

    for g in (n2 // nr - 2, n2 // nr - 1):
        t2_out(g).wait()
    for n in (n3 - 2, n3 - 1):
        t3_out(n).wait()
    for i in range(len(zeros)):
        zero_copy(i).wait()
    for i in range(2 * NSUM):
        arrived(db_ref.at[pl.ds(i * BLK, BLK)], dbr.at[i])

    for cond, make, _ in sends:
        if cond is None:
            make().wait_send()
        else:
            @pl.when(cond)
            def _():
                make().wait_send()

    @pl.loop(0, nv)
    def _(v):
        for dd, make in b_moves:
            @pl.when(d == dd)
            def _():
                make(v).wait_send()

    def sent(cp):
        cp.wait_send()

    for i in range(L_CUT):
        ly_do(i, sent)

    @pl.loop(0, ne)
    def _(e):
        @pl.when(is_root)
        def _():
            l_do(qc, e, 0, right, sent)
            l_do(qc, e, 1, left, sent)
            l_do(qc, e, 2, sib, sent)
            l_do(1 - qc, e, 2, sib, sent)

        @pl.when(jnp.logical_and(on_ring, jnp.logical_not(is_root)))
        def _():
            for q in range(2):
                l_fwd(q, e, sent)
                l_do(q, e, 2, sib, sent)

    @pl.loop(0, 8)
    def _(o):
        @pl.when(jnp.logical_not(is_root))
        def _():
            for part in range(2):
                sum_send(o, part).wait_send()

        @pl.when(jnp.logical_and(is_root, o != 0))
        def _():
            for b in range(NSUM):
                out_send(o, b, piece(o)).wait_send()


def solution(mesh):
    nr = mesh.shape["row"]
    nc = mesh.shape["col"]
    spec = P(("batch", "row"), "col")

    def per_device(lower_tri, right_side, grad_out):
        rows, cols = lower_tri.shape
        width = right_side.shape[1]
        ch = 2 * BLK
        nq, nb = rows // ch, cols // BLK
        nt = sum(nq - b for b in range(NSUM, nb))
        ntot = sum(nq - b for b in range(nb))
        yrows = rows - NSUM * ch
        nzero = nb * (nb - 1) // 2
        sd = jax.ShapeDtypeStruct
        outs = (sd((rows, width), BF), sd((rows, cols), BF), sd((nc, rows, width), BF), sd((nb, nc, BLK, width), BF),
                sd((nr, yrows, width), BF), sd((2, nr, nt, BLK, ch), BF),
                sd((nc, NSUM * BLK - SUM_UP, width), F32), sd((nc, SUM_UP, width), F32))
        vm = pltpu.VMEM
        dma = pltpu.SemaphoreType.DMA
        scratch = [vm((L_BUF, ch, BLK), BF), vm((nt, BLK, ch), BF), vm((NSUM * BLK, rows), BF), vm((2, rows, width), BF), vm((nc, NSUM * BLK, width), F32),
                   vm((NSUM * BLK - SUM_UP, width), F32), vm((SUM_UP, width), F32), vm((nc, NSUM * BLK, width), BF),
                   vm((nr, yrows, width), BF), vm((2, ch, (nq - NSUM) * ch), BF), vm((ch, width), F32), vm((2, ch, width), BF),
                   vm((2, ch, nc * width), BF), vm((2, BLK, nc * width), BF), vm((ch, BLK), F32), vm((2, ch, BLK), BF),
                   dma((14,)), dma((nc, 2)), dma((nb, 2)), dma((nb, nc)), dma((nb * B_CUT, 2)), dma((nb * B_CUT, 2)),
                   dma((6,)), dma((nr, 2)), dma((L_CUT,)), dma((nr * L_CUT, 2, 3)), dma((2, nr, L_CUT)),
                   dma((nc, 2)), dma((nc, 2)), dma((nc, NSUM)), dma((2 * NSUM,)),
                   dma((2, nr, 2)), dma((L_BUF,)), dma((2,)), dma((2,)), dma((nr,)), dma((2, 2, nq - NSUM)), dma((2,)), dma((2, nc)), dma((2, nc)),
                   dma((2,)), dma((nzero,)), dma((nb,))]
        res = pl.pallas_call(
            functools.partial(_kernel, nr, nc),
            out_shape=outs,
            in_specs=[pl.BlockSpec(memory_space=pl.ANY)] * 3,
            out_specs=tuple(pl.BlockSpec(memory_space=pl.ANY) for _ in outs),
            scratch_shapes=scratch,
            compiler_params=pltpu.CompilerParams(collective_id=0, has_side_effects=True, vmem_limit_bytes=67043328),
            name="tri_backward",
        )(lower_tri, right_side, grad_out)
        return res[0], res[1]

    return jax.shard_map(per_device, mesh=mesh, in_specs=(spec, spec, spec), out_specs=(spec, spec), check_vma=False)
```

time: 533 us -> 389 us (0.73)
  the two profiles are of different devices: /device:TPU:118 before, /device:TPU:97 now
where the time goes in v2:
time: 389 us; the launch traced here: 387 us
  Pallas kernels  372 us (96%)
  local copies, waits for them, and re-layouts  14.7 us (4%)
    pallas_call x1, Pallas kernels, per_device(): pl.pallas_call(functools.partial(_kernel, nr, nc), out_shape=outs, in_spe...  372 us
    unnamed x2, local copies, waits for them, and re-layouts  14.7 us

profile of v2, /device:TPU:97, one launch (start us, length us, event | category | flops | bytes accessed | tf_op | source)
XLA Modules:
  0.0 387.4 jit_solution(16518160570065539047)
XLA Ops:
  0.6 372.0 %tri_backward.1 = (bf16[3584,512]{1,0:T(8,128)(2,1)}, bf16[3584,1792]{1,0:T(8,128)(2,1)}, bf16[8,3584,512]{2,1,0:T(8,128)(2,1)}, bf16[7,8,256,512]{3,2,1,0:T(8,1...) custom-call(bf16[3584,1792]{1,0:T(8,128)(2,1)} %l_ref.1, ...), custom_call_target="tpu_custom_call" | custom-call | tf_op jit(solution)/shard_map/tri_backward/pallas_call | solution.py:890
  372.7 4.1 %copy.7 = bf16[3584,512]{1,0:T(8,128)(2,1)} copy(bf16[3584,512]{1,0:T(8,128)(2,1)} %get-tuple-element.8) | data formatting | bytes 7340032
  376.8 10.6 %copy.8 = bf16[3584,1792]{1,0:T(8,128)(2,1)} copy(bf16[3584,1792]{1,0:T(8,128)(2,1)} %get-tuple-element.9) | data formatting | bytes 25690112

commit v3 on v2

--- a/solution.py
+++ b/solution.py
@@ -1,4 +1,5 @@
 import functools
+import itertools
 
 import jax
 import jax.numpy as jnp
@@ -9,24 +10,25 @@
 
 BLK = 256
 NSUM = 3
+VMEM_BYTES = 67043328
 BF = jnp.bfloat16
 F32 = jnp.float32
 
+LATE = 4
 B_CUT = 4
 L_CUT = 3
 L_BUF = 4
-DX_SEND = 20
-DX_EVENTS = (28, 38, 42, 52, 61, 82)
-SUM_X = (7, 9, 43, 47, 55, 57, 88, 97)
-SUM_LINES = ((38, 50, 4), (73, 33, 4), (74, 40, 4))
-BX_LINE = (9, 37, 4)
-B_LINES = ((24, 16, 4), (40, 14, 4), (90, 8, 4), (99, 7, 4))
-L_LINES = ((49, 6, 4), (84, 14, 4), (91, 13, 4), (95, 13, 4))
-Y_EVENTS = (10, 15, 12, 55, 55, 65, 72)
-T2_A = 125
-T3_A = 98
-PER_SLOT = 2
-JA, JC, SUM_UP = 3, 4, 64
+DX_SEND = 14
+DX_EVENTS = (17, 33, 30, 46, 59, 73)
+SUM_X = (10, 11, 34, 36, 50, 53, 78, 86)
+SUM_LINES = ((28, 41, 4), (44, 42, 4), (62, 35, 4), (74, 39, 4))
+BX_LINE = (6, 31, 4)
+B_LINES = ((25, 13, 4), (37, 15, 4), (73, 11, 4), (82, 10, 4))
+L_LINES = ((45, 4, 4), (89, 11, 4), (90, 14, 4), (99, 11, 4))
+Y_EVENTS = (12, 12, 21, 50, 51, 63, 64)
+T2_A = 119
+T3_A = 88
+JA, JC, SUM_UP = 3,5,128
 
 
 def _line(line, n):
@@ -34,10 +36,111 @@
     return tuple(first + i * num // den for i in range(n))
 
 
+def _round_lower(acc, out, b, q, row, col):
+    part = BLK // 2
+    for i in range(acc.shape[0] // part):
+        pos = lax.broadcasted_iota(jnp.int32, (part, BLK), 0) + i * part
+        rg = ((2 * q + i * part // BLK) * row[1] + row[0]) * BLK + pos % BLK
+        cg = (b * col[1] + col[0]) * BLK + lax.broadcasted_iota(jnp.int32, (part, BLK), 1)
+        out[pl.ds(i * part, part)] = jnp.where(rg >= cg, acc[pl.ds(i * part, part)], 0.0).astype(BF)
+
+
+def _last_kernel(nr, nc, x_ref, dxg, bc, tiles_in, db_in, db_ref, dl_ref, xt, bt, tiles, dbv, acc, made, zero,
+                 s_x, s_b, s_in, s_out, s_made, s_zero, s_db):
+    rows, cols = dl_ref.shape
+    width = x_ref.shape[1]
+    ch = 2 * BLK
+    nq, nb = rows // ch, cols // BLK
+    r = lax.axis_index("row")
+    c = lax.axis_index("col")
+    early = [(b, q) for b in range(LATE) for q in range(b, nq)]
+    late = [(b, q) for q in range(LATE, nq) for b in range(LATE, min(q + 1, nb))]
+    above = [(b, q) for b in range(nb) for q in range(b)]
+
+    def place(b, q):
+        return dl_ref.at[pl.ds(pl.multiple_of(q * ch, ch), ch), pl.ds(pl.multiple_of(b * BLK, BLK), BLK)]
+
+    def x_load(q, o):
+        j = lax.rem(c + o, nc)
+        rws = pl.ds(pl.multiple_of((LATE + q) * ch, ch), ch)
+        src = x_ref.at[rws] if o == 0 else dxg.at[j, rws]
+        return pltpu.make_async_copy(src, xt.at[q, :, pl.ds(pl.multiple_of(j * width, width), width)], s_x.at[q, o])
+
+    def b_load(b, j):
+        return pltpu.make_async_copy(bc.at[LATE + b, j], bt.at[b, :, pl.ds(j * width, width)], s_b.at[b, j])
+
+    def tile_load(n):
+        return pltpu.make_async_copy(tiles_in.at[n], tiles.at[n], s_in.at[n])
+
+    def tile_store(n):
+        return pltpu.make_async_copy(tiles.at[n], place(*early[n]), s_out.at[n])
+
+    def zero_store(n):
+        return pltpu.make_async_copy(zero, place(*above[n]), s_zero.at[n])
+
+    db_load = pltpu.make_async_copy(db_in, dbv, s_db.at[0])
+    db_store = pltpu.make_async_copy(dbv, db_ref, s_db.at[1])
+    for i in range(nq - LATE):
+        for o in range(nc):
+            x_load(i, o).start()
+        for j in range(nc):
+            b_load(i, j).start()
+    for n in range(len(early)):
+        tile_load(n).start()
+    db_load.start()
+    zero[...] = jnp.zeros_like(zero)
+    for n in range(len(above)):
+        zero_store(n).start()
+
+    def of(n, vals):
+        v = jnp.int32(vals[0])
+        for i in range(1, len(vals)):
+            v = jnp.where(n >= i, vals[i], v)
+        return v
+
+    def made_store(n):
+        return pltpu.make_async_copy(made.at[n], place(of(n, [b for b, _ in late]), of(n, [q for _, q in late])), s_made.at[n])
+
+    @pl.loop(0, len(late))
+    def _(n):
+        b = of(n, [b for b, _ in late])
+        q = of(n, [q for _, q in late])
+
+        @pl.when(b == LATE)
+        def _():
+            for o in range(nc):
+                x_load(q - LATE, o).wait()
+
+        @pl.when(b == q)
+        def _():
+            for j in range(nc):
+                b_load(b - LATE, j).wait()
+
+        acc[...] = lax.dot_general(xt[q - LATE], bt[b - LATE], (((1,), (1,)), ((), ())), preferred_element_type=F32)
+        _round_lower(acc, made.at[n], b, q, (r, nr), (c, nc))
+        made_store(n).start()
+
+        @pl.when(n == len(late) // 2)
+        def _():
+            for i in range(len(early)):
+                tile_load(i).wait()
+                tile_store(i).start()
+            db_load.wait()
+            db_store.start()
+
+    for n in range(len(late)):
+        made_store(n).wait()
+    for n in range(len(early)):
+        tile_store(n).wait()
+    for n in range(len(above)):
+        zero_store(n).wait()
+    db_store.wait()
+
+
 def _kernel(nr, nc, l_ref, b_ref, x_ref, db_ref, dl_ref, dxg, bc, dxt, ltg, prm, prp,
             lt_in, ltv, lth, dxv, pv, rbm, rbp, sv, dxtv, ltb, acc2, o2, dt, bv, acc3, o3,
             dxs, dxr, bxs, bxr, bys, byr, dys, dyr, lys, lts, ltr, prs, prr, dbs, dbr,
-            s_ltz, s_lin, s_dxv, s_rb, s_dxt, s_ltb, s_o2, s_dt, s_bv, s_o3, s_zero, s_own):
+            s_ltz, s_lin, s_dxv, s_rb, s_dxt, s_ltb, s_o2, s_dt, s_bv, s_o3, s_own):
     rows, cols = l_ref.shape
     width = x_ref.shape[1]
     ch = 2 * BLK
@@ -110,6 +213,11 @@
                 v = jnp.where(n >= i, vals[i], v)
         return v
 
+    def summed(u):
+        if isinstance(u, int):
+            return u % (nc - 1) + 1 if u else 0
+        return jnp.where(u == 0, 0, lax.rem(u, nc - 1) + 1)
+
     def block_of(n, order):
         return table(n, [b for b, _ in order]), table(n, [q for _, q in order])
 
@@ -150,15 +258,16 @@
     def dx_wait(p, h):
         arrived(dxg.at[p, pl.ds(h * half, half)], dxr.at[p, h])
 
-    own_list = [functools.partial(dx_own, hf, second, 0), functools.partial(dx_own, hf, sib, 4),
-                functools.partial(dx_own, hs, second, 1), functools.partial(dx_own, hs, sib, 5),
-                functools.partial(dx_own, hs, first, 2), functools.partial(dx_own, hf, first, 3)]
-    ev = [(first, hf, [functools.partial(dx_fwd, first, hf, second, 6), functools.partial(dx_fwd, first, hf, sib, 7)]),
-          (first, hs, [functools.partial(dx_fwd, first, hs, sib, 8)]),
-          (second, hs, [functools.partial(dx_fwd, second, hs, first, 9), functools.partial(dx_fwd, second, hs, sib, 10)]),
-          (second, hf, [functools.partial(dx_fwd, second, hf, sib, 11)]),
-          (far, hf, [functools.partial(dx_fwd, far, hf, sib, 12)]),
-          (far, hs, [functools.partial(dx_fwd, far, hs, sib, 13)])]
+    dx_id = itertools.count()
+    own_list = [functools.partial(dx_own, hf, second, next(dx_id)), functools.partial(dx_own, hf, sib, next(dx_id)),
+                functools.partial(dx_own, hs, second, next(dx_id)), functools.partial(dx_own, hs, sib, next(dx_id)),
+                functools.partial(dx_own, hs, first, next(dx_id)), functools.partial(dx_own, hf, first, next(dx_id))]
+    ev = [(first, hf, [functools.partial(dx_fwd, first, hf, second, next(dx_id)), functools.partial(dx_fwd, first, hf, sib, next(dx_id))]),
+          (first, hs, [functools.partial(dx_fwd, first, hs, sib, next(dx_id))]),
+          (second, hs, [functools.partial(dx_fwd, second, hs, first, next(dx_id)), functools.partial(dx_fwd, second, hs, sib, next(dx_id))]),
+          (second, hf, [functools.partial(dx_fwd, second, hf, sib, next(dx_id))]),
+          (far, hf, [functools.partial(dx_fwd, far, hf, sib, next(dx_id))]),
+          (far, hs, [functools.partial(dx_fwd, far, hs, sib, next(dx_id))])]
     for m in own_list:
         note(None, m)
     for _, _, ms in ev:
@@ -180,9 +289,10 @@
     def dy_wait(p, h):
         arrived(dxt.at[p, pl.ds(h * yhalf, yhalf)], dyr.at[p, h])
 
-    dy_list = [functools.partial(dy_own, 0, up, 0), functools.partial(dy_own, 1, down, 1),
-               functools.partial(dy_own, 1, up, 2), functools.partial(dy_own, 0, down, 3),
-               functools.partial(dy_fwd, down, 0, up, 4), functools.partial(dy_fwd, up, 1, down, 5)]
+    dy_id = itertools.count()
+    dy_list = [functools.partial(dy_own, 0, up, next(dy_id)), functools.partial(dy_own, 1, down, next(dy_id)),
+               functools.partial(dy_own, 1, up, next(dy_id)), functools.partial(dy_own, 0, down, next(dy_id)),
+               functools.partial(dy_fwd, down, 0, up, next(dy_id)), functools.partial(dy_fwd, up, 1, down, next(dy_id))]
     for m in dy_list:
         note(None, m)
 
@@ -200,21 +310,15 @@
     load_x(0, 0).start()
 
     def own_b(b):
-        return pltpu.make_async_copy(b_ref.at[pl.ds((2 * b + qc) * BLK, BLK)], sv.at[b, pl.ds(0, BLK)], s_own.at[b])
+        return pltpu.make_async_copy(b_ref.at[pl.ds((2 * b + qc) * BLK, BLK)], sv.at[summed(b), pl.ds(0, BLK)], s_own.at[b])
 
     def own_b_out(b):
-        return pltpu.make_async_copy(sv.at[b, pl.ds(0, BLK)], bc.at[b, c], bxr.at[b, c])
+        return pltpu.make_async_copy(sv.at[summed(b), pl.ds(0, BLK)], bc.at[b, c], bxr.at[b, c])
 
     @pl.when(is_root)
     def _():
         for b in range(nb):
             own_b(b).start()
-
-    zeros = [(b, q) for b in range(nb) for q in range(b)]
-
-    def zero_copy(i):
-        b, q = zeros[i]
-        return pltpu.make_async_copy(lt_in.at[0], dl_ref.at[pl.ds(q * ch, ch), pl.ds(b * BLK, BLK)], s_zero.at[i])
 
     order = tail + head
     ntot = len(order)
@@ -302,8 +406,6 @@
 
     lt_in[...] = jnp.zeros_like(lt_in)
     l_zeros(lambda cp: cp.start())
-    for i in range(len(zeros)):
-        zero_copy(i).start()
 
     @pl.when(is_root)
     def _():
@@ -493,9 +595,9 @@
             o2[lax.rem(g, 2)] = acc2[...].astype(BF)
             t2_out(g).start()
 
-    t3_order = [(b, q) for b in range(nb) for q in range(b, nq)]
+    t3_order = [(b, q) for b in range(LATE) for q in range(b, nq)]
     n3 = len(t3_order)
-    t3_last = [max(n for n, (bb, _) in enumerate(t3_order) if bb == b) for b in range(nb)]
+    t3_last = [max(n for n, (bb, _) in enumerate(t3_order) if bb == b) for b in range(LATE)]
 
     def t3_load(n, o):
         b, q = block_of(n, t3_order)
@@ -509,10 +611,8 @@
         return pltpu.make_async_copy(bc.at[b, j], bv.at[k, :, pl.ds(j * width, width)], s_bv.at[k, j])
 
     def t3_out(n):
-        b, q = block_of(n, t3_order)
         k = lax.rem(n, 2)
-        dst = dl_ref.at[pl.ds(pl.multiple_of(q * ch, ch), ch), pl.ds(pl.multiple_of(b * BLK, BLK), BLK)]
-        return pltpu.make_async_copy(o3.at[k], dst, s_o3.at[k])
+        return pltpu.make_async_copy(o3.at[k], dl_ref.at[n], s_o3.at[k])
 
     def t3_item(n):
         b, q = block_of(n, t3_order)
@@ -536,38 +636,28 @@
         def _():
             t3_out(n - 2).wait()
 
-        for i in range(ch // 128):
-            pos = lax.broadcasted_iota(jnp.int32, (128, BLK), 0) + i * 128
-            kpos = lax.broadcasted_iota(jnp.int32, (128, BLK), 1)
-            rg = ((2 * q + i * 128 // BLK) * nr + r) * BLK + pos % BLK
-            cg = (b * nc + c) * BLK + kpos
-            o3[k, pl.ds(i * 128, 128)] = jnp.where(rg >= cg, acc3[pl.ds(i * 128, 128)], 0.0).astype(BF)
+        _round_lower(acc3, o3.at[k], b, q, (r, nr), (c, nc))
         t3_out(n).start()
     b_ready = [max(x[B_CUT * b + B_CUT - 1] for x in b_slot) for b in range(nb)]
     l_ready = [max(x[nr * i + nr - 1] for x in l_slot) for i in range(L_CUT)]
     t2_need = [l_ready[min(w // nr + 1, L_CUT - 1)] for w in range(n2)]
 
-    def b_loads(slots):
-        return [max(b_ready[b], T3_A - 1 if b < 2 else slots[t3_last[b - 2]]) for b in range(nb)]
-
-    def earliest(begin, end, n, fits):
-        found = []
-        for first in range(begin, end):
-            num = next((m for m in range(2, BLK) if fits(_line((first, m, 4), n))), None)
-            if num is not None:
-                found.append((_line((first, num, 4), n)[-1], first, num))
-        _, first, num = min(found)
-        return first, num, _line((first, num, 4), n)
-
-    t2_first_slot, t2_num, t2_slots = earliest(T2_A, T2_A + 2, n2, lambda x: all(x[w] >= t2_need[min(w + 1, n2 - 1)] for w in range(n2)))
-    t3_first_slot, t3_num, t3_slots = earliest(
-        max(T3_A, b_ready[0] + 1), max(T3_A, b_ready[1]) + 2, n3,
-        lambda x: all(a > y for a, y in zip((x[t3_last[b] + b - nb + 1] for b in range(nb)), b_loads(x))))
-    bv_slots = b_loads(t3_slots)
+    def packed(start, ready):
+        out = []
+        for n in range(len(ready)):
+            out.append(max(start, ready[n], out[-1] + 1 if out else 0))
+        return out
+
+    t2_slots = packed(T2_A, t2_need[1:] + t2_need[-1:])
+    t3_slots, bv_slots = [], []
+    for b in range(LATE):
+        bv_slots.append(max(b_ready[b], T3_A - 1 if b < 2 else t3_slots[t3_last[b - 2]]))
+        t3_slots = packed(T3_A, t3_slots + [bv_slots[b] + 1] * (nq - b))
     assert T2_A > max(l_ready[1], Y_EVENTS[6]) and Y_EVENTS[6] > max(Y_EVENTS[3:6])
     assert T3_A > max(load_x_at[-1], DX_EVENTS[-1])
-    lists = ((SUM_X,) + sum_at, b_slot, l_slot)
-    assert all(a < b for f in lists for x in f for a, b in zip(x[:-1], x[1:]))
+    lists = (sum_at, b_slot, l_slot)
+    assert all(a < b for f in lists + ((SUM_X,),) for x in f for a, b in zip(x[:-1], x[1:]))
+    assert all(sum_at[0][u] > SUM_X[summed(u)] for u in range(nc))
     assert all(a < b for f in lists for y, z in zip(f[:-1], f[1:]) for a, b in zip(y, z))
     assert all(SUM_X[o - 2] < load_x_at[o] for o in range(2, nc))
     assert all(max(DX_EVENTS[o:o + 2]) <= load_x_at[o + 2] for o in (0, 2, 4))
@@ -577,6 +667,9 @@
     down_depth = nr - 1 - d
     up_depth = mod(d - 1, nr)
     off_ring = jnp.logical_not(on_ring)
+
+    def listed(vals):
+        return lambda n: table(n, tuple(vals) + (slots,))
 
     events = []
 
@@ -646,27 +739,22 @@
     n_first = len(events)
     event(T2_A - 1, t2_first)
     event(T3_A - 1, t3_first)
-    for b in range(nb):
+    for b in range(LATE):
         event(bv_slots[b], functools.partial(bv_event, b))
-    masks = {}
-    for i, (x, _) in enumerate(events):
-        masks[x] = masks.get(x, 0) + (1 << i)
-
-    def mask_of(s):
-        m = jnp.int32(0)
-        for x in sorted(masks):
-            m = jnp.where(s == x, masks[x], m)
-        return m
-
-    def run_events(mask, lo, hi):
-        part = sum(1 << i for i in range(lo, hi))
-
-        @pl.when(jnp.bitwise_and(mask, part) != 0)
-        def _():
+
+    def event_flow(lo, hi):
+        part = sorted(range(lo, hi), key=lambda i: events[i][0])
+        at = sorted({events[i][0] for i in part})
+        masks = [sum(1 << (i - lo) for i in part if events[i][0] == x) for x in at]
+
+        def run(k):
+            mask = table(k, masks)
             for i in range(lo, hi):
-                @pl.when(jnp.bitwise_and(mask, 1 << i) != 0)
+                @pl.when(jnp.bitwise_and(mask, 1 << (i - lo)) != 0)
                 def _():
                     events[i][1]()
+
+        return listed(at), len(at), run
 
     def b_due(v):
         @pl.when(is_root)
@@ -711,8 +799,16 @@
         def _():
             l_stage1(e)
 
-    def sum_due(o, part, depth):
-        sum_step(o, part, depth)
+    def sum_due(u, part, depth):
+        o = summed(u)
+
+        @pl.when(depth == 0)
+        def _():
+            sum_send(o, part).start()
+
+        @pl.when(depth > 0)
+        def _():
+            sum_step(o, part, depth)
 
     def load_due(o):
         p = piece(o)
@@ -730,82 +826,54 @@
     def part_due(o):
         load_x(0, lax.rem(o, 2)).wait()
         partial(o)
-        for part, depth in ((0, down_depth), (1, up_depth)):
-            @pl.when(depth == 0)
-            def _():
-                sum_send(o, part).start()
-
-    def stage(lines, k):
+
+    def stage(lines, k, total):
         first = jnp.int32(slots)
         num = jnp.int32(0)
         for i, (f, m, _) in enumerate(lines):
             first = jnp.where(k == i, f, first)
             num = jnp.where(k == i, m, num)
-        return lambda n: first + n * num // 4
-
-    def listed(vals):
-        return lambda n: table(n, vals + (slots,))
-
-    def up_due(o):
-        sum_due(o, 1, up_depth)
+        return lambda n: jnp.where(n < total, first + n * num // 4, slots)
+
+    def up_due(u):
+        sum_due(u, 1, up_depth)
 
         @pl.when(is_root)
         def _():
-            finish(o)
+            finish(summed(u))
 
     none = jnp.int32(-1)
-    flows = [(stage(L_LINES, jnp.where(is_root, 0, jnp.where(off_ring, 3, 1))), ne, l_due),
-             (stage(L_LINES, jnp.where(is_root, 2, none)), ne, l_stage2),
-             (stage(B_LINES, jnp.where(d == 0, 0, jnp.where(d == 2, 2, 1))), nv, b_due),
-             (stage(B_LINES, jnp.where(d == 1, 3, none)), nv, b_last),
-             (stage(SUM_LINES, down_depth - 1), nc, lambda o: sum_due(o, 0, down_depth)),
-             (stage(SUM_LINES, up_depth - 1), nc, up_due),
-             (listed(load_x_at), nc, load_due),
-             (listed(SUM_X), nc, part_due)]
-    work = [(lambda n: t2_first_slot + n * t2_num // 4, n2, t2_item), (lambda n: t3_first_slot + n * t3_num // 4, n3, t3_item)]
+    flows = [event_flow(0, n_first)[::2],
+             (stage(L_LINES, jnp.where(is_root, 0, jnp.where(off_ring, 3, 1)), ne), l_due),
+             (stage(L_LINES, jnp.where(is_root, 2, none), ne), l_stage2),
+             (stage(B_LINES, jnp.where(d == 0, 0, jnp.where(d == 2, 2, 1)), nv), b_due),
+             (stage(B_LINES, jnp.where(d == 1, 3, none), nv), b_last),
+             (stage(SUM_LINES, down_depth, nc), lambda u: sum_due(u, 0, down_depth)),
+             (stage(SUM_LINES, up_depth, nc), up_due),
+             (listed(load_x_at), load_due),
+             (listed(SUM_X), part_due),
+             event_flow(n_first, n_first + 2)[::2],
+             (listed(t2_slots), t2_item), (listed(t3_slots), t3_item), event_flow(n_first + 2, len(events))[::2]]
 
     def slot(s, carry):
-        nxt = list(carry)
-        mask = mask_of(s)
-        run_events(mask, 0, n_first)
-
-        def due(i, when, total, fn):
-            n = nxt[i]
-            hit = jnp.logical_and(n < total, when(n) == s)
-
-            @pl.when(hit)
-            def _():
+        nxt = []
+        for (when, fn), (n, at) in zip(flows, carry):
+            def go(n, fn=fn, when=when):
                 fn(n)
-
-            nxt[i] = jnp.where(hit, n + 1, n)
-
-        for i, (when, total, fn) in enumerate(flows):
-            due(i, when, total, fn)
-        run_events(mask, n_first, n_first + 2)
-        for i, (when, total, fn) in enumerate(work):
-            k = len(flows) + i
-
-            def again(_, n):
-                hit = jnp.logical_and(n < total, when(n) == s)
-
-                @pl.when(hit)
-                def _():
-                    fn(n)
-
-                return jnp.where(hit, n + 1, n)
-
-            nxt[k] = lax.fori_loop(0, PER_SLOT, again, nxt[k])
-        run_events(mask, n_first + 2, len(events))
+                return n + 1, when(n + 1)
+
+            def stay(n, at=at):
+                return n, at
+
+            nxt.append(lax.cond(at == s, go, stay, n))
         return tuple(nxt)
 
-    lax.fori_loop(0, slots, slot, tuple(jnp.int32(0) for _ in range(len(flows) + len(work))))
+    lax.fori_loop(0, slots, slot, tuple((jnp.int32(0), jnp.int32(when(jnp.int32(0)))) for when, _ in flows))
 
     for g in (n2 // nr - 2, n2 // nr - 1):
         t2_out(g).wait()
     for n in (n3 - 2, n3 - 1):
         t3_out(n).wait()
-    for i in range(len(zeros)):
-        zero_copy(i).wait()
     for i in range(2 * NSUM):
         arrived(db_ref.at[pl.ds(i * BLK, BLK)], dbr.at[i])
 
@@ -871,9 +939,10 @@
         nt = sum(nq - b for b in range(NSUM, nb))
         ntot = sum(nq - b for b in range(nb))
         yrows = rows - NSUM * ch
-        nzero = nb * (nb - 1) // 2
         sd = jax.ShapeDtypeStruct
-        outs = (sd((rows, width), BF), sd((rows, cols), BF), sd((nc, rows, width), BF), sd((nb, nc, BLK, width), BF),
+        n_early = sum(nq - b for b in range(LATE))
+        n_late = sum(nq - b for b in range(LATE, nb))
+        outs = (sd((rows, width), BF), sd((n_early, ch, BLK), BF), sd((nc, rows, width), BF), sd((nb, nc, BLK, width), BF),
                 sd((nr, yrows, width), BF), sd((2, nr, nt, BLK, ch), BF),
                 sd((nc, NSUM * BLK - SUM_UP, width), F32), sd((nc, SUM_UP, width), F32))
         vm = pltpu.VMEM
@@ -886,16 +955,29 @@
                    dma((6,)), dma((nr, 2)), dma((L_CUT,)), dma((nr * L_CUT, 2, 3)), dma((2, nr, L_CUT)),
                    dma((nc, 2)), dma((nc, 2)), dma((nc, NSUM)), dma((2 * NSUM,)),
                    dma((2, nr, 2)), dma((L_BUF,)), dma((2,)), dma((2,)), dma((nr,)), dma((2, 2, nq - NSUM)), dma((2,)), dma((2, nc)), dma((2, nc)),
-                   dma((2,)), dma((nzero,)), dma((nb,))]
+                   dma((2,)), dma((nb,))]
         res = pl.pallas_call(
             functools.partial(_kernel, nr, nc),
             out_shape=outs,
             in_specs=[pl.BlockSpec(memory_space=pl.ANY)] * 3,
             out_specs=tuple(pl.BlockSpec(memory_space=pl.ANY) for _ in outs),
             scratch_shapes=scratch,
-            compiler_params=pltpu.CompilerParams(collective_id=0, has_side_effects=True, vmem_limit_bytes=67043328),
+            compiler_params=pltpu.CompilerParams(collective_id=0, has_side_effects=True, vmem_limit_bytes=VMEM_BYTES),
             name="tri_backward",
         )(lower_tri, right_side, grad_out)
-        return res[0], res[1]
+        db, tiles, dxg, bc = res[:4]
+        far = nq - LATE
+        return pl.pallas_call(
+            functools.partial(_last_kernel, nr, nc),
+            out_shape=(sd((rows, width), BF), sd((rows, cols), BF)),
+            in_specs=[pl.BlockSpec(memory_space=pl.ANY)] * 5,
+            out_specs=(pl.BlockSpec(memory_space=pl.ANY),) * 2,
+            scratch_shapes=[vm((far, ch, nc * width), BF), vm((far, BLK, nc * width), BF), vm((n_early, ch, BLK), BF), vm((rows, width), BF),
+                            vm((ch, BLK), F32), vm((n_late, ch, BLK), BF), vm((ch, BLK), BF),
+                            dma((far, nc)), dma((far, nc)), dma((n_early,)), dma((n_early,)), dma((n_late,)),
+                            dma((nb * (nb - 1) // 2,)), dma((2,))],
+            compiler_params=pltpu.CompilerParams(vmem_limit_bytes=VMEM_BYTES),
+            name="tri_backward_last",
+        )(grad_out, dxg, bc, tiles, db)
 
     return jax.shard_map(per_device, mesh=mesh, in_specs=(spec, spec, spec), out_specs=(spec, spec), check_vma=False)

time: 389 us -> 370 us (0.951)
  local copies, waits for them, and re-layouts: 14.7 us -> 0 us
  Pallas kernels: 372 us -> 368 us
    pallas_call x1, Pallas kernels: 372 us -> 351 us  [per_device(): pl.pallas_call(functools.partial(_kernel, nr, nc), out_shape=outs, in_spe...]
    pallas_call x0 -> x1, Pallas kernels: none -> 16.5 us  [per_device(): pl.pallas_call(functools.partial(_last_kernel, nr, nc), out_shape=(sd((ro...]
    unnamed x2 -> x0, local copies, waits for them, and re-layouts: 14.7 us -> none
where the time goes in v3:
time: 370 us; the launch traced here: 368 us
  Pallas kernels  368 us (99%)
    pallas_call x1, Pallas kernels, per_device(): pl.pallas_call(functools.partial(_kernel, nr, nc), out_shape=outs, in_spe...  351 us
    pallas_call x1, Pallas kernels, per_device(): pl.pallas_call(functools.partial(_last_kernel, nr, nc), out_shape=(sd((ro...  16.5 us

profile of v3, /device:TPU:97, one launch (start us, length us, event | category | flops | bytes accessed | tf_op | source)
XLA Modules:
  0.0 368.4 jit_solution(2260754049875149527)
XLA Ops:
  0.6 351.2 %tri_backward.1 = (bf16[3584,512]{1,0:T(8,128)(2,1)}, bf16[22,512,256]{2,1,0:T(8,128)(2,1)}, bf16[8,3584,512]{2,1,0:T(8,128)(2,1)}, bf16[7,8,256,512]{3,2,1,0:T(...) custom-call(bf16[3584,1792]{1,0:T(8,128)(2,1)} %l_ref.1, ...), custom_call_target="tpu_custom_call" | custom-call | tf_op jit(solution)/shard_map/tri_backward/pallas_call | solution.py:959
  351.9 16.5 %tri_backward_last.1 = (bf16[3584,512]{1,0:T(8,128)(2,1)}, bf16[3584,1792]{1,0:T(8,128)(2,1)}) custom-call(bf16[3584,512]{1,0:T(8,128)(2,1)} %x_ref.3, bf16[8,3584,512]{2,1,0:T(8,128)(2,1)} %get-tuple-element.6.dxg, bf16[7,8,256,512]{3,2,1,0:T(8,128)(2,1)} %get-tuple-element.7.bc, bf16[22,512,256]{2,1,0:T(8,128)(2,1)} %get-tuple-element.8.tiles_in, ...), custom_call_target="tpu_custom_call" | custom-call | tf_op jit(solution)/shard_map/tri_backward_last/pallas_call | solution.py:970

commit v4 on v3

--- a/solution.py
+++ b/solution.py
@@ -17,18 +17,19 @@
 LATE = 4
 B_CUT = 4
 L_CUT = 3
+SUM_CUT = 2
 L_BUF = 4
-DX_SEND = 14
-DX_EVENTS = (17, 33, 30, 46, 59, 73)
-SUM_X = (10, 11, 34, 36, 50, 53, 78, 86)
-SUM_LINES = ((28, 41, 4), (44, 42, 4), (62, 35, 4), (74, 39, 4))
+DX_SEND = 17
+DX_EVENTS = (17, 34, 32, 52, 59, 73)
+SUM_X = (10, 11, 35, 36, 53, 54, 77, 85)
+SUM_LINES = ((29, 20, 4), (45, 20, 4), (52, 20, 4), (65, 20, 4))
 BX_LINE = (6, 31, 4)
-B_LINES = ((25, 13, 4), (37, 15, 4), (73, 11, 4), (82, 10, 4))
-L_LINES = ((45, 4, 4), (89, 11, 4), (90, 14, 4), (99, 11, 4))
+B_LINES = ((24, 15, 4), (35, 16, 4), (72, 11, 4), (81, 10, 4))
+L_LINES = ((43, 4, 4), (87, 11, 4), (92, 12, 4), (98, 11, 4))
 Y_EVENTS = (12, 12, 21, 50, 51, 63, 64)
 T2_A = 119
-T3_A = 88
-JA, JC, SUM_UP = 3,5,128
+T3_A = 92
+JA, JC, SUM_UP = 3, 5, 128
 
 
 def _line(line, n):
@@ -161,7 +162,7 @@
     nv = nb * B_CUT
     ne = nr * L_CUT
     load_x_at = tuple(max(x - 1, 0) for x in SUM_X)
-    sum_at = tuple(_line(x, nc) for x in SUM_LINES)
+    sum_at = tuple(_line(x, nc * SUM_CUT) for x in SUM_LINES)
     bx_at = _line(BX_LINE, nb)
     b_slot = tuple(_line(x, nv) for x in B_LINES)
     l_slot = tuple(_line(x, ne) for x in L_LINES)
@@ -492,31 +493,32 @@
 
     mrow = SUM_UP
     prows = NSUM * BLK
-    part_rows = ((mrow, prows - mrow), (0, mrow))
-
-    def sum_send(o, part):
-        lo, n = part_rows[part]
-        to = row_of(mod(d - 1, nr)) if part == 0 else row_of(mod(d + 1, nr))
-        dst = (prm if part == 0 else prp).at[o]
-        return remote(pv.at[o, pl.ds(lo, n)], dst, prs.at[o, part], prr.at[o, part], dev(to, c))
-
-    def sum_step(o, part, depth):
-        lo, n = part_rows[part]
-        land = (prm if part == 0 else prp).at[o]
-        buf = rbm if part == 0 else rbp
-
-        arrived(land, prr.at[o, part])
-        cp = pltpu.make_async_copy(land, buf, s_rb.at[part])
+    hrow = (prows - mrow) // SUM_CUT
+
+    def sum_parts(o, i):
+        if i is None:
+            return pv.at[o, pl.ds(0, mrow)], prp.at[o], rbp, SUM_CUT
+        return pv.at[o, pl.ds(pl.multiple_of(mrow + i * hrow, 16), hrow)], prm.at[o, i], rbm, i
+
+    def sum_send(o, i):
+        src, dst, _, k = sum_parts(o, i)
+        to = row_of(mod(d + (1 if i is None else -1), nr))
+        return remote(src, dst, prs.at[o, k], prr.at[o, k], dev(to, c))
+
+    def sum_step(o, i):
+        own, land, buf, k = sum_parts(o, i)
+        arrived(land, prr.at[o, k])
+        cp = pltpu.make_async_copy(land, buf, s_rb.at[0 if i is None else 1])
         cp.start()
         cp.wait()
 
-        @pl.loop(0, n // 64)
-        def _(i):
-            pv[o, pl.ds(lo + i * 64, 64)] = pv[o, pl.ds(lo + i * 64, 64)] + buf[pl.ds(i * 64, 64)]
+        @pl.loop(0, buf.shape[0] // 16)
+        def _(j):
+            own[pl.ds(j * 16, 16)] = own[pl.ds(j * 16, 16)] + buf[pl.ds(j * 16, 16)]
 
         @pl.when(jnp.logical_not(is_root))
         def _():
-            sum_send(o, part).start()
+            sum_send(o, i).start()
 
     def out_send(o, b, to):
         dst = db_ref.at[pl.ds((2 * b + qc) * BLK, BLK)]
@@ -657,11 +659,11 @@
     assert T3_A > max(load_x_at[-1], DX_EVENTS[-1])
     lists = (sum_at, b_slot, l_slot)
     assert all(a < b for f in lists + ((SUM_X,),) for x in f for a, b in zip(x[:-1], x[1:]))
-    assert all(sum_at[0][u] > SUM_X[summed(u)] for u in range(nc))
+    assert all(sum_at[0][u * SUM_CUT] > SUM_X[summed(u)] for u in range(nc))
     assert all(a < b for f in lists for y, z in zip(f[:-1], f[1:]) for a, b in zip(y, z))
     assert all(SUM_X[o - 2] < load_x_at[o] for o in range(2, nc))
     assert all(max(DX_EVENTS[o:o + 2]) <= load_x_at[o + 2] for o in (0, 2, 4))
-    assert all(b_slot[0][B_CUT * b] <= sum_at[-1][b] for b in range(nb))
+    assert all(b_slot[0][B_CUT * b] <= sum_at[-1][b * SUM_CUT + SUM_CUT - 1] for b in range(nb))
     slots = 1 + max(t3_slots[-1], t2_slots[-1], sum_at[-1][-1], b_ready[-1], l_ready[-1])
 
     down_depth = nr - 1 - d
@@ -799,16 +801,17 @@
         def _():
             l_stage1(e)
 
-    def sum_due(u, part, depth):
-        o = summed(u)
-
+    def sum_due(o, i, depth):
         @pl.when(depth == 0)
         def _():
-            sum_send(o, part).start()
+            sum_send(o, i).start()
 
         @pl.when(depth > 0)
         def _():
-            sum_step(o, part, depth)
+            sum_step(o, i)
+
+    def down_due(n):
+        sum_due(summed(n // SUM_CUT), lax.rem(n, SUM_CUT), down_depth)
 
     def load_due(o):
         p = piece(o)
@@ -836,7 +839,7 @@
         return lambda n: jnp.where(n < total, first + n * num // 4, slots)
 
     def up_due(u):
-        sum_due(u, 1, up_depth)
+        sum_due(summed(u), None, up_depth)
 
         @pl.when(is_root)
         def _():
@@ -848,8 +851,8 @@
              (stage(L_LINES, jnp.where(is_root, 2, none), ne), l_stage2),
              (stage(B_LINES, jnp.where(d == 0, 0, jnp.where(d == 2, 2, 1)), nv), b_due),
              (stage(B_LINES, jnp.where(d == 1, 3, none), nv), b_last),
-             (stage(SUM_LINES, down_depth, nc), lambda u: sum_due(u, 0, down_depth)),
-             (stage(SUM_LINES, up_depth, nc), up_due),
+             (stage(SUM_LINES, down_depth, nc * SUM_CUT), down_due),
+             (lambda n: stage(SUM_LINES, up_depth, nc * SUM_CUT)(n * SUM_CUT + SUM_CUT - 1), up_due),
              (listed(load_x_at), load_due),
              (listed(SUM_X), part_due),
              event_flow(n_first, n_first + 2)[::2],
@@ -917,8 +920,8 @@
     def _(o):
         @pl.when(jnp.logical_not(is_root))
         def _():
-            for part in range(2):
-                sum_send(o, part).wait_send()
+            for i in (None,) + tuple(range(SUM_CUT)):
+                sum_send(o, i).wait_send()
 
         @pl.when(jnp.logical_and(is_root, o != 0))
         def _():
@@ -944,16 +947,16 @@
         n_late = sum(nq - b for b in range(LATE, nb))
         outs = (sd((rows, width), BF), sd((n_early, ch, BLK), BF), sd((nc, rows, width), BF), sd((nb, nc, BLK, width), BF),
                 sd((nr, yrows, width), BF), sd((2, nr, nt, BLK, ch), BF),
-                sd((nc, NSUM * BLK - SUM_UP, width), F32), sd((nc, SUM_UP, width), F32))
+                sd((nc, SUM_CUT, (NSUM * BLK - SUM_UP) // SUM_CUT, width), F32), sd((nc, SUM_UP, width), F32))
         vm = pltpu.VMEM
         dma = pltpu.SemaphoreType.DMA
         scratch = [vm((L_BUF, ch, BLK), BF), vm((nt, BLK, ch), BF), vm((NSUM * BLK, rows), BF), vm((2, rows, width), BF), vm((nc, NSUM * BLK, width), F32),
-                   vm((NSUM * BLK - SUM_UP, width), F32), vm((SUM_UP, width), F32), vm((nc, NSUM * BLK, width), BF),
+                   vm(((NSUM * BLK - SUM_UP) // SUM_CUT, width), F32), vm((SUM_UP, width), F32), vm((nc, NSUM * BLK, width), BF),
                    vm((nr, yrows, width), BF), vm((2, ch, (nq - NSUM) * ch), BF), vm((ch, width), F32), vm((2, ch, width), BF),
                    vm((2, ch, nc * width), BF), vm((2, BLK, nc * width), BF), vm((ch, BLK), F32), vm((2, ch, BLK), BF),
                    dma((14,)), dma((nc, 2)), dma((nb, 2)), dma((nb, nc)), dma((nb * B_CUT, 2)), dma((nb * B_CUT, 2)),
                    dma((6,)), dma((nr, 2)), dma((L_CUT,)), dma((nr * L_CUT, 2, 3)), dma((2, nr, L_CUT)),
-                   dma((nc, 2)), dma((nc, 2)), dma((nc, NSUM)), dma((2 * NSUM,)),
+                   dma((nc, SUM_CUT + 1)), dma((nc, SUM_CUT + 1)), dma((nc, NSUM)), dma((2 * NSUM,)),
                    dma((2, nr, 2)), dma((L_BUF,)), dma((2,)), dma((2,)), dma((nr,)), dma((2, 2, nq - NSUM)), dma((2,)), dma((2, nc)), dma((2, nc)),
                    dma((2,)), dma((nb,))]
         res = pl.pallas_call(

time: 370 us -> 365 us (0.986)
  Pallas kernels: 368 us -> 363 us
    pallas_call x1, Pallas kernels: 351 us -> 347 us  [per_device(): pl.pallas_call(functools.partial(_kernel, nr, nc), out_shape=outs, in_spe...]
where the time goes in v4:
time: 365 us; the launch traced here: 364 us
  Pallas kernels  363 us (99%)
    pallas_call x1, Pallas kernels, per_device(): pl.pallas_call(functools.partial(_kernel, nr, nc), out_shape=outs, in_spe...  347 us
    pallas_call x1, Pallas kernels, per_device(): pl.pallas_call(functools.partial(_last_kernel, nr, nc), out_shape=(sd((ro...  16.5 us

profile of v4, /device:TPU:97, one launch (start us, length us, event | category | flops | bytes accessed | tf_op | source)
XLA Modules:
  0.0 363.9 jit_solution(11988571170800492190)
XLA Ops:
  0.6 346.7 %tri_backward.1 = (bf16[3584,512]{1,0:T(8,128)(2,1)}, bf16[22,512,256]{2,1,0:T(8,128)(2,1)}, bf16[8,3584,512]{2,1,0:T(8,128)(2,1)}, bf16[7,8,256,512]{3,2,1,0:T(...) custom-call(bf16[3584,1792]{1,0:T(8,128)(2,1)} %l_ref.1, ...), custom_call_target="tpu_custom_call" | custom-call | tf_op jit(solution)/shard_map/tri_backward/pallas_call | solution.py:962
  347.3 16.5 %tri_backward_last.1 = (bf16[3584,512]{1,0:T(8,128)(2,1)}, bf16[3584,1792]{1,0:T(8,128)(2,1)}) custom-call(bf16[3584,512]{1,0:T(8,128)(2,1)} %x_ref.3, bf16[8,3584,512]{2,1,0:T(8,128)(2,1)} %get-tuple-element.6.dxg, bf16[7,8,256,512]{3,2,1,0:T(8,128)(2,1)} %get-tuple-element.7.bc, bf16[22,512,256]{2,1,0:T(8,128)(2,1)} %get-tuple-element.8.tiles_in, ...), custom_call_target="tpu_custom_call" | custom-call | tf_op jit(solution)/shard_map/tri_backward_last/pallas_call | solution.py:973

commit v5 on v4

--- a/solution.py
+++ b/solution.py
@@ -19,17 +19,17 @@
 L_CUT = 3
 SUM_CUT = 2
 L_BUF = 4
-DX_SEND = 17
-DX_EVENTS = (17, 34, 32, 52, 59, 73)
-SUM_X = (10, 11, 35, 36, 53, 54, 77, 85)
-SUM_LINES = ((29, 20, 4), (45, 20, 4), (52, 20, 4), (65, 20, 4))
-BX_LINE = (6, 31, 4)
-B_LINES = ((24, 15, 4), (35, 16, 4), (72, 11, 4), (81, 10, 4))
-L_LINES = ((43, 4, 4), (87, 11, 4), (92, 12, 4), (98, 11, 4))
-Y_EVENTS = (12, 12, 21, 50, 51, 63, 64)
-T2_A = 119
-T3_A = 92
-JA, JC, SUM_UP = 3, 5, 128
+DX_SEND = 24
+DX_EVENTS = (26, 35, 39, 59, 67, 74)
+SUM_X = (12, 13, 36, 37, 60, 61, 79, 80)
+SUM_LINES = ((31, 20, 4), (45, 20, 4), (54, 20, 4), (65, 20, 4))
+BX_LINE = (8, 31, 4)
+B_LINES = ((21, 15, 4), (32, 16, 4), (69, 11, 4), (80, 10, 4))
+L_LINES = ((38, 6, 4), (82, 13, 4), (90, 13, 4), (99, 10, 4))
+Y_EVENTS = (12, 14, 24, 50, 51, 70, 71)
+T2_A = 122
+T3_A = 80
+JA, JC, SUM_UP = 3, (5, 4), 128
 
 
 def _line(line, n):
@@ -486,10 +486,17 @@
     def b_wait(v, lo, hi, rs):
         arrived(b_ref_of(v, lo, hi), byr.at[v, rs])
 
-    ja, jc = JA, JC
-    b_moves = [(0, lambda v: b_send(v, 0, nc, 0, 0, 3)), (0, lambda v: b_send(v, ja, nc, 1, 0, 1)),
-               (3, lambda v: b_send(v, 0, jc, 0, 0, 2)), (1, lambda v: b_send(v, jc, nc, 0, 1, 2)),
-               (2, lambda v: b_send(v, 0, ja, 0, 1, 1))]
+    ja = JA
+
+    def by_share(v, fn):
+        for k, jc in enumerate(JC):
+            @pl.when(lax.rem(v, len(JC)) == k)
+            def _():
+                fn(jc)
+
+    b_moves = [(0, lambda v, jc: b_send(v, 0, nc, 0, 0, 3)), (0, lambda v, jc: b_send(v, ja, nc, 1, 0, 1)),
+               (3, lambda v, jc: b_send(v, 0, jc, 0, 0, 2)), (1, lambda v, jc: b_send(v, jc, nc, 0, 1, 2)),
+               (2, lambda v, jc: b_send(v, 0, ja, 0, 1, 1))]
 
     mrow = SUM_UP
     prows = NSUM * BLK
@@ -766,24 +773,24 @@
                 @pl.loop(0, nc)
                 def _(j):
                     arrived(bc.at[v // B_CUT, j], bxr.at[v // B_CUT, j])
-            b_moves[0][1](v).start()
-            b_moves[1][1](v).start()
+            b_moves[0][1](v, nc).start()
+            b_moves[1][1](v, nc).start()
 
         @pl.when(d == 3)
         def _():
             b_wait(v, 0, nc, 0)
-            b_moves[2][1](v).start()
+            by_share(v, lambda jc: b_moves[2][1](v, jc).start())
 
         @pl.when(d == 1)
         def _():
             b_wait(v, ja, nc, 0)
-            b_moves[3][1](v).start()
+            by_share(v, lambda jc: b_moves[3][1](v, jc).start())
 
         @pl.when(d == 2)
         def _():
-            b_wait(v, 0, jc, 0)
-            b_moves[4][1](v).start()
-            b_wait(v, jc, nc, 1)
+            by_share(v, lambda jc: b_wait(v, 0, jc, 0))
+            b_moves[4][1](v, nc).start()
+            by_share(v, lambda jc: b_wait(v, jc, nc, 1))
 
     def b_last(v):
         b_wait(v, 0, ja, 1)
@@ -893,7 +900,7 @@
         for dd, make in b_moves:
             @pl.when(d == dd)
             def _():
-                make(v).wait_send()
+                by_share(v, lambda jc: make(v, jc).wait_send())
 
     def sent(cp):
         cp.wait_send()

time: 365 us -> 357 us (0.978)
  Pallas kernels: 363 us -> 354 us
    pallas_call x1, Pallas kernels: 347 us -> 337 us  [per_device(): pl.pallas_call(functools.partial(_kernel, nr, nc), out_shape=outs, in_spe...]
where the time goes in v5:
time: 357 us; the launch traced here: 354 us
  Pallas kernels  354 us (99%)
    pallas_call x1, Pallas kernels, per_device(): pl.pallas_call(functools.partial(_kernel, nr, nc), out_shape=outs, in_spe...  337 us
    pallas_call x1, Pallas kernels, per_device(): pl.pallas_call(functools.partial(_last_kernel, nr, nc), out_shape=(sd((ro...  16.5 us

profile of v5, /device:TPU:97, one launch (start us, length us, event | category | flops | bytes accessed | tf_op | source)
XLA Modules:
  0.0 354.2 jit_solution(2793380631275311285)
XLA Ops:
  0.6 337.1 %tri_backward.1 = (bf16[3584,512]{1,0:T(8,128)(2,1)}, bf16[22,512,256]{2,1,0:T(8,128)(2,1)}, bf16[8,3584,512]{2,1,0:T(8,128)(2,1)}, bf16[7,8,256,512]{3,2,1,0:T(...) custom-call(bf16[3584,1792]{1,0:T(8,128)(2,1)} %l_ref.1, ...), custom_call_target="tpu_custom_call" | custom-call | tf_op jit(solution)/shard_map/tri_backward/pallas_call | solution.py:969
  337.7 16.5 %tri_backward_last.1 = (bf16[3584,512]{1,0:T(8,128)(2,1)}, bf16[3584,1792]{1,0:T(8,128)(2,1)}) custom-call(bf16[3584,512]{1,0:T(8,128)(2,1)} %x_ref.3, bf16[8,3584,512]{2,1,0:T(8,128)(2,1)} %get-tuple-element.6.dxg, bf16[7,8,256,512]{3,2,1,0:T(8,128)(2,1)} %get-tuple-element.7.bc, bf16[22,512,256]{2,1,0:T(8,128)(2,1)} %get-tuple-element.8.tiles_in, ...), custom_call_target="tpu_custom_call" | custom-call | tf_op jit(solution)/shard_map/tri_backward_last/pallas_call | solution.py:980
